TPU v7x, 32 devices: a 4x4x1 block of a 4x4x8 slice. The times are simulated.
32 devices in a mesh: rep: 1 (over z), head: 4 (over y), seq: 8 (over x, core).
Axes of the slice: x: 4, y: 4, z: 1, core: 2. Of those that a mesh axis runs over, the one named last changes fastest.
The devices are a block of a 4x4x8 slice.
Arguments:
- tokens: bfloat16 [64, 6144], P('rep')
- w_query: bfloat16 [6144, 6144], replicated
- w_key: bfloat16 [6144, 1024], replicated
- w_value: bfloat16 [6144, 1024], replicated
- w_out: bfloat16 [6144, 6144], P(('head', 'seq'))
- k_cache: bfloat16 [64, 2048, 8, 128], P('rep', 'seq', 'head')
- v_cache: bfloat16 [64, 2048, 8, 128], P('rep', 'seq', 'head')
- positions: int32 [64], P('rep')
Outputs:
- output 1: bfloat16 [64, 6144], P('rep')
- output 2: bfloat16 [64, 2048, 8, 128], P('rep', 'seq', 'head')
- output 3: bfloat16 [64, 2048, 8, 128], P('rep', 'seq', 'head')
All inputs are finite; a program needn't handle non-finite values.
Results may differ from a plain program's by a relative error of at most 0.00793011.
Values are sent between devices in bfloat16 or wider.
A program may use at most 768 MiB of HBM per device.

v0:
```python
import jax
import jax.numpy as jnp
from jax import lax
from jax.sharding import PartitionSpec as P


def solution(mesh):
    head_devs = mesh.shape['head']
    cache_spec = P('rep', 'seq', 'head', None)

    def local_step(tokens, w_query, w_key, w_value, w_out, k_cache, v_cache, positions):
        batch_size, shard_len, kv_local, head_dim = k_cache.shape
        heads_total = w_query.shape[1] // head_dim
        groups = heads_total // (kv_local * head_devs)
        q_cols = kv_local * groups * head_dim
        kv_cols = kv_local * head_dim
        wo_rows = w_out.shape[0]
        head_idx = lax.axis_index('head')
        seq_idx = lax.axis_index('seq')
        wq_local = lax.dynamic_slice_in_dim(w_query, head_idx * q_cols, q_cols, axis=1)
        wk_local = lax.dynamic_slice_in_dim(w_key, head_idx * kv_cols, kv_cols, axis=1)
        wv_local = lax.dynamic_slice_in_dim(w_value, head_idx * kv_cols, kv_cols, axis=1)
        query = jnp.dot(tokens, wq_local, preferred_element_type=jnp.float32).astype(jnp.bfloat16).reshape(batch_size, kv_local, groups, head_dim)
        new_key = jnp.dot(tokens, wk_local, preferred_element_type=jnp.float32).astype(jnp.bfloat16).reshape(batch_size, 1, kv_local, head_dim)
        new_value = jnp.dot(tokens, wv_local, preferred_element_type=jnp.float32).astype(jnp.bfloat16).reshape(batch_size, 1, kv_local, head_dim)
        slot_ids = seq_idx * shard_len + jnp.arange(shard_len, dtype=jnp.int32)
        is_slot = (slot_ids[None, :] == positions[:, None])[:, :, None, None]
        k_new = jnp.where(is_slot, new_key, k_cache)
        v_new = jnp.where(is_slot, new_value, v_cache)
        scores = jnp.einsum('bkgd,btkd->bkgt', query, k_new, preferred_element_type=jnp.float32) * head_dim ** -0.5
        valid_mask = (slot_ids[None, :] <= positions[:, None])[:, None, None, :]
        scores = jnp.where(valid_mask, scores, -jnp.inf)
        local_max = jnp.max(scores, axis=-1)
        safe_max = jnp.where(jnp.isfinite(local_max), local_max, 0.0)
        weights = jnp.exp(scores - safe_max[..., None])
        local_sum = jnp.sum(weights, axis=-1)
        local_mix = jnp.einsum('bkgt,btkd->bkgd', weights.astype(jnp.bfloat16), v_new, preferred_element_type=jnp.float32)
        global_max = lax.pmax(local_max, 'seq')
        rescale = jnp.exp(local_max - global_max)
        total_sum, total_mix = lax.psum((local_sum * rescale, local_mix * rescale[..., None]), 'seq')
        attn_flat = (total_mix / total_sum[..., None]).astype(jnp.bfloat16).reshape(batch_size, q_cols)
        attn_part = lax.dynamic_slice_in_dim(attn_flat, seq_idx * wo_rows, wo_rows, axis=1)
        y_part = jnp.dot(attn_part, w_out, preferred_element_type=jnp.float32)
        y_total = lax.psum(y_part, ('head', 'seq'))
        return y_total.astype(jnp.bfloat16), k_new, v_new

    return jax.shard_map(
        local_step,
        mesh=mesh,
        in_specs=(P('rep', None), P(), P(), P(), P(('head', 'seq'), None), cache_spec, cache_spec, P('rep')),
        out_specs=(P('rep', None), cache_spec, cache_spec),
        check_vma=False,
    )
```

profile of v0, /device:TPU:97, one launch (start us, length us, event | category | flops | bytes accessed | tf_op | source)
XLA Modules:
  0.0 206.6 jit_solution(2892275189105540509)
XLA Ops:
  7.2 0.0 copy-start
  7.2 0.1 all-reduce.3.cloned.1.call-start
  7.3 2.9 %fusion.34 = bf16[64,256]{1,0:T(8,128)(2,1)S(1)} fusion(bf16[64,6144]{1,0:T(8,128)(2,1)} %param.8, bf16[6144,1024]{1,0:T(8,128)(2,1)} %param.10, s32[]{:T(128)S(6)} %select_n.30), kind=kOutput, calls=%fused_computation.20 | convolution fusion | flops 201342976 | bytes 3964932 | tf_op jit(solution)/shard_map/dot_general | solution.py:24
  10.2 2.8 %fusion.31 = bf16[64,256]{1,0:T(8,128)(2,1)S(1)} fusion(bf16[64,6144]{1,0:T(8,128)(2,1)} %param.8, bf16[6144,1024]{1,0:T(8,128)(2,1)} %param.11, s32[]{:T(128)S(6)} %select_n.30), kind=kOutput, calls=%fused_computation.19 | convolution fusion | flops 201342976 | bytes 3964932 | tf_op jit(solution)/shard_map/dot_general | solution.py:25
  13.0 0.0 copy-start.4
  13.0 10.0 %fusion.13 = bf16[64,1536]{1,0:T(8,128)(2,1)S(1)} fusion(bf16[64,6144]{1,0:T(8,128)(2,1)} %param.8, bf16[6144,6144]{1,0:T(8,128)(2,1)} %param.9, s32[]{:T(128)S(6)} %select_n.29), kind=kOutput, calls=%fused_computation.13 | convolution fusion | flops 1208057856 | bytes 19857412 | tf_op jit(solution)/shard_map/dot_general | solution.py:23
  23.0 0.9 reshape.75
  23.9 0.0 copy-done.4
  23.9 0.1 broadcast_compare_fusion.1
  24.0 0.0 copy-start.2
  24.0 25.6 %broadcast_select_fusion.1 = (bf16[64,256,2,128]{3,2,1,0:T(2,128)(2,1)S(1)}, bf16[64,256,2,128]{3,2,1,0:T(2,128)(2,1)}) fusion(bf16[64,256,2,128]{3,2,1,0:T(2,128)(2,1)} %param.13, pred[64,256]{1,0:T(8,128)(4,1)S(1)} %get-tuple-element.8, bf16[64,2,128]{2,1,0:T(2,128)(2,1)S(1)} %broadcast_in_dim.55, bf16[64,256,2,128]{3,2,1,0:T(2,128)(2,1)} %param.14, ...), kind=kLoop, calls=%fused_computation.3 | loop fusion | flops 8388608 | bytes 33636352 | tf_op jit(solution)/shard_map/jit(_where)/select_n | solution.py:28
  49.7 0.0 copy-start.1
  49.7 3.4 %copy-done.1 = bf16[64,256,2,128]{3,2,1,0:T(2,128)(2,1)} copy-done((bf16[64,256,2,128]{3,2,1,0:T(2,128)(2,1)}, bf16[64,256,2,128]{3,2,1,0:T(2,128)(2,1)S(1)}, u32[]{:S(2)}) %copy-start.1) | copy-done | bytes 8388632
  53.1 0.0 copy-done.2
  53.1 2.4 %fusion.48 = (f32[64,2,6]{2,1,0:T(2,128)S(1)}, f32[64,2,6,256]{3,2,1,0:T(8,128)S(1)}) fusion(bf16[64,2,6,128]{3,2,1,0:T(8,128)(2,1)S(1)} %copy-done.2, bf16[64,256,2,128]{3,2,1,0:T(2,128)(2,1)S(1)} %get-tuple-element.5, pred[64,256]{1,0:T(8,128)(4,1)S(1)} %get-tuple-element.7), kind=kOutput, calls=%fused_computation.38 | convolution fusion | flops 50920704 | bytes 9391104 | tf_op jit(solution)/shard_map/bkgd,btkd->bkgt/dot_general | solution.py:30
  55.5 0.0 copy-start.3
  55.5 25.1 %pmax.7 = f32[64,2,6]{2,1,0:T(2,128)} all-reduce(f32[64,2,6]{2,1,0:T(2,128)S(1)} %get-tuple-element.9), channel_id=1, replica_groups=mesh['rep'=1,'head'=4,'seq'=8] {'seq'}, use_global_device_ids=true, to_apply=%region_1.2 | all-reduce | flops 768 | bytes 6144 | tf_op jit(solution)/shard_map/pmax | solution.py:38
  80.6 0.4 fusion.37
  81.0 0.0 copy-done.3
  81.0 0.9 fusion.47
  81.9 5.5 %fusion.22 = f32[64,2,6,128]{3,2,1,0:T(8,128)} fusion(bf16[64,256,2,128]{3,2,1,0:T(2,128)(2,1)} %get-tuple-element.6, f32[64,2,6,256]{3,2,1,0:T(8,128)S(1)} %get-tuple-element.10, f32[64,2,6]{2,1,0:T(2,128)} %copy-done.3, f32[64,2,6]{2,1,0:T(2,128)S(1)} %bitcast.20), kind=kOutput, calls=%fused_computation.16 | convolution fusion | flops 50823168 | bytes 9574400 | tf_op jit(solution)/shard_map/bkgt,btkd->bkgd/dot_general | solution.py:37
  87.4 0.1 all-reduce.3.cloned.1.call-update
  87.4 25.0 %psum.22 = f32[64,2,6]{2,1,0:T(2,128)S(1)} all-reduce(f32[64,2,6]{2,1,0:T(2,128)S(1)} %bitcast.18), channel_id=1, replica_groups=mesh['rep'=1,'head'=4,'seq'=8] {'seq'}, use_global_device_ids=true, to_apply=%region_4.5 | all-reduce | flops 768 | bytes 6144 | tf_op jit(solution)/shard_map/psum | solution.py:40
  112.4 32.1 %all-reduce.3.cloned.1.call-done = f32[64,2,6,128]{3,2,1,0:T(8,128)} async-done(((f32[64,2,6,128]{3,2,1,0:T(8,128)}), f32[64,2,6,128]{3,2,1,0:T(8,128)}) %all-reduce.3.cloned.1.call-update) | async-done | bytes 393232 | tf_op jit(solution)/shard_map/psum | solution.py:40
  144.6 1.2 divide_convert_fusion
  145.8 0.2 reshape.76
  146.1 0.0 copy-done
  146.1 1.8 fusion.41
  147.8 51.9 %all-reduce.4 = bf16[64,6144]{1,0:T(8,128)(2,1)} all-reduce(f32[64,6144]{1,0:T(8,128)} %fusion.41), channel_id=1, replica_groups=mesh['rep'=1,'head'=4,'seq'=8] {'head','seq'}, use_global_device_ids=true, to_apply=%region_5.6 | all-reduce | flops 393216 | bytes 2359296 | tf_op jit(solution)/shard_map/psum | solution.py:44
  (4 shorter events, 0.1 us)
Async XLA Ops:
  7.2 138.9 %copy-start = (bf16[192,6144]{1,0:T(8,128)(2,1)S(1)}, bf16[192,6144]{1,0:T(8,128)(2,1)}, u32[]{:S(2)}) copy-start(bf16[192,6144]{1,0:T(8,128)(2,1)} %param.12) | copy-start | bytes 7077892
  7.2 137.4 %all-reduce.3.cloned.1.call-start = ((), (), s32[]{:S(2)}) async-start(), calls=%async_computation | async-start | bytes 1048576 | tf_op jit(solution)/shard_map/psum | solution.py:40
  13.0 10.9 %copy-start.4 = (s32[64]{0:T(128)S(1)}, s32[64]{0:T(128)}, u32[]{:S(2)}) copy-start(s32[64]{0:T(128)} %param.15) | copy-start | bytes 772
  24.0 29.1 %copy-start.2 = (bf16[64,2,6,128]{3,2,1,0:T(8,128)(2,1)S(1)}, bf16[64,2,6,128]{3,2,1,0:T(8,128)(2,1)}, u32[]{:S(2)}) copy-start(bf16[64,2,6,128]{3,2,1,0:T(8,128)(2,1)} %reshape.75) | copy-start | bytes 589828
  49.7 3.4 %copy-start.1 = (bf16[64,256,2,128]{3,2,1,0:T(2,128)(2,1)}, bf16[64,256,2,128]{3,2,1,0:T(2,128)(2,1)S(1)}, u32[]{:S(2)}) copy-start(bf16[64,256,2,128]{3,2,1,0:T(2,128)(2,1)S(1)} %get-tuple-element.5) | copy-start | bytes 25165828
  55.5 25.5 %copy-start.3 = (f32[64,2,6]{2,1,0:T(2,128)}, f32[64,2,6]{2,1,0:T(2,128)S(1)}, u32[]{:S(2)}) copy-start(f32[64,2,6]{2,1,0:T(2,128)S(1)} %is-finite_select_fusion) | copy-start | bytes 9220
Sparse Core Ops, SparseCore 0:
  87.6 56.9 all-reduce.2
where the time goes:
time: 207 us
  blocking collectives  102 us (49%)
  waiting for transfers between devices  32.2 us (16%)
  other arithmetic  28.3 us (14%)
  matrix products  25.3 us (12%)
  between operations  14.2 us (7%)
  local copies, waits for them, and re-layouts  4.63 us (2%)
    psum x1, blocking collectives, local_step(): y_total = lax.psum(y_part, ('head', 'seq'))  51.9 us
    psum x1, waiting for transfers between devices, local_step(): lax.psum((local_sum * rescale, local_mix * rescale[..., None]), 'seq')  32.1 us
    select_n x1, other arithmetic, local_step(): k_new = jnp.where(is_slot, new_key, k_cache)  25.6 us
    pmax x1, blocking collectives, local_step(): global_max = lax.pmax(local_max, 'seq')  25.1 us
    psum x1, blocking collectives, local_step(): lax.psum((local_sum * rescale, local_mix * rescale[..., None]), 'seq')  25 us
    dot_general x1, matrix products, local_step(): jnp.dot(tokens, wq_local, preferred_element_type=jnp.float32)  9.95 us
    dot_general x1, matrix products, local_step(): jnp.einsum('bkgt,btkd->bkgd', weights.astype(jnp.bfloat16), v_new, prefer...  5.5 us
  transfers between devices with their start and end apart: 1, of which 1 were waited for; matrix products, arithmetic and copies ran while one was open for 0% of the time, Pallas kernels for 0%

commit v1 on v0

v1 whole, which is shorter than its diff:
```python
import functools

import jax
import jax.numpy as jnp
from jax import lax
from jax.experimental import pallas as pl
from jax.experimental.pallas import tpu as pltpu
from jax.sharding import PartitionSpec as P

MESH = pl.DeviceIdType.MESH
BF16 = jnp.bfloat16
F32 = jnp.float32
PAD = 16
NB = 8


def attend(groups, tok, wq, wk, wv, kc, vc, pos, ko, vo, acch, stat,
           wbuf, kb, vb, pj, q2, accs, wsem, ksem, vsem, kosem, vosem):
    head = lax.axis_index('head')
    seq = lax.axis_index('seq')
    batch, rows, dim = kc.shape
    shard = rows // 2
    heads = 2 * groups
    nq = groups
    width = 2 * dim
    steps = batch // NB

    def weight(i):
        if i < nq:
            src = wq.at[:, pl.ds(pl.multiple_of((head * nq + i) * width, width), width)]
        else:
            src = (wk if i == nq else wv).at[:, pl.ds(pl.multiple_of(head * width, width), width)]
        return pltpu.make_async_copy(src, wbuf.at[i], wsem.at[i])

    def block(src, dst, sem, c):
        span = pl.ds(pl.multiple_of(c * NB, NB), NB)
        return pltpu.make_async_copy(src.at[span], dst.at[span], sem.at[c])

    for i in range(nq + 2):
        weight(i).start()
    for c in range(steps):
        block(kc, kb, ksem, c).start()
        block(vc, vb, vsem, c).start()
    q2[...] = jnp.zeros_like(q2)

    def project(i, carry):
        pltpu.make_async_copy(wq.at[:, pl.ds(0, width)], wbuf.at[i], wsem.at[i]).wait()
        out = jnp.dot(tok[...], wbuf[i], preferred_element_type=F32)
        pj[i] = out.astype(BF16).astype(F32)
        return carry

    lax.fori_loop(0, nq + 2, project, 0)
    for h in range(heads):
        q2[pl.ds(h, batch, stride=PAD), :] = pj[h // 2][:, (h % 2) * dim:(h % 2 + 1) * dim]

    row16 = lax.broadcasted_iota(jnp.int32, (16, dim), 0)
    even = (row16 & 1) == 0
    lane = lax.broadcasted_iota(jnp.int32, (PAD, dim), 1)
    col = lax.broadcasted_iota(jnp.int32, (PAD, rows), 1)
    rid = lax.broadcasted_iota(jnp.int32, (PAD, rows), 0)
    slot = col >> 1
    own = jnp.where(rid < groups, 0, jnp.where(rid < heads, 1, 2)) == (col & 1)
    slot = jnp.where(own, slot, jnp.int32(1 << 30))

    def step(c, st):
        def update(buf, which):
            for i in range(NB):
                b = c * NB + i
                t = pos[b] - seq * shard
                inside = (t >= 0) & (t < shard)
                tc = jnp.clip(t, 0, shard - 1)
                start = pl.multiple_of((tc >> 3) * 16, 16)
                hit = ((row16 >> 1) == (tc & 7)) & inside
                new = pj[which, pl.ds(b, 1), :]
                new = jnp.where(even, new[:, :dim], new[:, dim:])
                old = buf[b, pl.ds(start, 16), :].astype(F32)
                buf[b, pl.ds(start, 16), :] = jnp.where(hit, new, old).astype(BF16)

        block(kc, kb, ksem, c).wait()
        update(kb, nq)
        block(kb, ko, kosem, c).start()
        block(vc, vb, vsem, c).wait()
        update(vb, nq + 1)
        block(vb, vo, vosem, c).start()
        for i in range(NB):
            b = c * NB + i
            t = pos[b] - seq * shard
            q = q2[pl.ds(pl.multiple_of(b * PAD, PAD), PAD), :].astype(BF16)
            s = lax.dot_general(q, kb[b], (((1,), (1,)), ((), ())), preferred_element_type=F32)
            s = jnp.where(slot <= t, s * dim ** -0.5, -jnp.inf)
            m = jnp.max(s, axis=-1, keepdims=True)
            w = jnp.exp(s - jnp.where(m == -jnp.inf, 0.0, m))
            l = jnp.sum(w, axis=-1, keepdims=True)
            acc = jnp.dot(w.astype(BF16), vb[b], preferred_element_type=F32)
            accs[pl.ds(pl.multiple_of(b * PAD, PAD), PAD), :] = acc
            st = jnp.where(lane == b, m, jnp.where(lane == b + batch, l, st))
        return st

    stat[...] = lax.fori_loop(0, steps, step, jnp.zeros((PAD, dim), F32))
    for h in range(heads):
        acch[h] = accs[pl.ds(h, batch, stride=PAD), :]
    for c in range(steps):
        block(kb, ko, kosem, c).wait()
        block(vb, vo, vosem, c).wait()


def finish(acch, stat, wo, out, wob, rx, srx, fs, lhs, yp, dx, z, r1, s1, r2, yb,
           osem, ds_s, ds_r, ss_s, ss_r, d_s, d_r, a_s, a_r, b_s, b_r, c_s, c_r, e_s, e_r, f_s, f_r):
    y = lax.axis_index('head')
    s = lax.axis_index('seq')
    ny = lax.axis_size('head')
    ns = lax.axis_size('seq')
    nx = ns // 2
    x = s // 2
    p = lax.rem(s, 2)
    heads, batch, dim = acch.shape
    wrows = wo.shape[0]
    wide = yp.shape[-1]
    half = batch // 2

    def at(yy, xx, pp):
        return {'head': yy, 'seq': xx * 2 + pp}

    partner = at(y, x, 1 - p)

    def on_x(k):
        return at(y, lax.rem(x + k, nx), p)

    def on_y(k):
        return at(lax.rem(y + k, ny), x, p)

    load = pltpu.make_async_copy(wo, wob.at[pl.ds(pl.multiple_of(p * (2 * dim - wrows), 64), wrows), :], osem)
    load.start()
    gap = pl.multiple_of((1 - p) * wrows, 64)
    wob[pl.ds(gap, 2 * dim - wrows), :] = jnp.zeros((2 * dim - wrows, wob.shape[1]), BF16)

    barrier = pltpu.get_barrier_semaphore()
    for k in range(1, ns):
        pl.semaphore_signal(barrier, inc=1, device_id={'head': y, 'seq': lax.rem(s + k, ns)}, device_id_type=MESH)
    for k in range(1, ny):
        pl.semaphore_signal(barrier, inc=1, device_id=on_y(k), device_id_type=MESH)
    pl.semaphore_wait(barrier, ns - 1 + ny - 1)

    def copy(src, dst, send, recv, dev):
        return pltpu.make_async_remote_copy(src_ref=src, dst_ref=dst, send_sem=send, recv_sem=recv,
                                            device_id=dev, device_id_type=MESH)

    def first(dest):
        return (dest // 2) * 3 + lax.rem(dest, 2)

    sends = []
    order = [4, 5, 3, 2, 6, 7, 1]
    for k in order:
        dest = lax.rem(s + k, ns)
        dev = {'head': y, 'seq': dest}
        cp = copy(stat, srx.at[k], ss_s.at[k], ss_r.at[k], dev)
        cp.start()
        sends.append(cp)
        cp = copy(acch.at[pl.ds(first(dest), 2)], rx.at[k], ds_s.at[k], ds_r.at[k], dev)
        cp.start()
        sends.append(cp)
    srx[0] = stat[...]
    fs[...] = jnp.zeros_like(fs)
    for cp in sends:
        cp.wait_recv()

    h0 = first(s)
    tiles = [srx[i, pl.ds(h0, 2), :] for i in range(ns)]
    top = functools.reduce(jnp.maximum, tiles)
    scale = [jnp.exp(t - top) for t in tiles]
    total = functools.reduce(lambda a, b: a + b, [e * pltpu.roll(t, dim // 2, 1) for e, t in zip(scale, tiles)])
    for i in range(ns):
        fs[2 * i:2 * i + 2, :] = scale[i] / total
    ft = jnp.transpose(fs[...])[:batch]
    lane = lax.broadcasted_iota(jnp.int32, (batch, dim), 1)
    for j in range(2):
        acc = ft[:, j:j + 1] * acch[h0 + j]
        for i in range(1, ns):
            acc = acc + ft[:, 2 * i + j:2 * i + j + 1] * rx[i, j]
        keep = (lane >= dim // 2) if j == 0 else (lane < dim // 2)
        keep = keep | (p == j)
        lhs[:, j * dim:(j + 1) * dim] = jnp.where(keep, acc, 0.0).astype(BF16)
    load.wait()

    seq_of = []
    for k in (2, 1, 3, 0):
        seq_of.append((0, k))
        seq_of.append((1, k))

    def block_of(side, k):
        return lax.rem(x + k, nx) if side == 0 else nx + lax.rem(y + k, ny)

    pair = {}
    for side, k in seq_of:
        c = block_of(side, k)
        v = jnp.dot(lhs[...], wob[:, pl.ds(pl.multiple_of(c * wide, wide), wide)], preferred_element_type=F32)
        i = side * 4 + k
        yp[i, 0] = v[:half]
        yp[i, 1] = v[half:]
        cp = copy(yp.at[i, 1 - p], dx.at[i], d_s.at[i], d_r.at[i], partner)
        cp.start()
        pair[side, k] = cp
        sends.append(cp)

    one = {}
    for side, k in seq_of:
        i = side * 4 + k
        pair[side, k].wait_recv()
        z[i] = yp[i, p] + dx[i]
        if k:
            cp = copy(z.at[i], r1.at[i], a_s.at[i], a_r.at[i], on_x(k) if side == 0 else on_y(k))
            cp.start()
            one[side, k] = cp
            sends.append(cp)

    two = {}
    for side in range(2):
        base = side * 4
        for k in range(1, 4):
            one[side, k].wait_recv()
        v = z[base] + r1[base + 1] + r1[base + 2] + r1[base + 3]
        for r in range(4):
            s1[side, r] = v[8 * r:8 * r + 8]
        for k in range(1, 4):
            dest = lax.rem(y + k, ny) if side == 0 else lax.rem(x + k, nx)
            cp = copy(s1.at[side, dest], r2.at[base + k], b_s.at[base + k], b_r.at[base + k],
                      on_y(k) if side == 0 else on_x(k))
            cp.start()
            two[side, k] = cp
            sends.append(cp)

    three = {}
    for side in range(2):
        base = side * 4
        mine = y if side == 0 else x
        c = block_of(side, 0)
        for k in range(1, 4):
            two[side, k].wait_recv()
        v = s1[side, mine] + r2[base + 1] + r2[base + 2] + r2[base + 3]
        row = 4 * p + mine
        yb[c, row] = v.astype(BF16)
        for k in range(1, 4):
            cp = copy(yb.at[c, row], yb.at[c, row], c_s.at[base + k], c_r.at[base + k],
                      on_y(k) if side == 0 else on_x(k))
            cp.start()
            three[side, k] = cp
            sends.append(cp)

    def mirror(side, k):
        c = block_of(side, k)
        part = yb.at[c, pl.ds(4 * p, 4)]
        i = side * 4 + k
        cp = copy(part, part, f_s.at[i], f_r.at[i], partner)
        cp.start()
        sends.append(cp)
        return cp

    four = {}
    last = []
    for side in range(2):
        base = side * 4
        c = block_of(side, 0)
        for k in range(1, 4):
            three[side, k].wait_recv()
        part = yb.at[c, pl.ds(4 * p, 4)]
        for k in range(1, 4):
            cp = copy(part, part, e_s.at[base + k], e_r.at[base + k], on_x(k) if side == 0 else on_y(k))
            cp.start()
            four[side, k] = cp
            sends.append(cp)
        last.append(mirror(side, 0))
    for k in (1, 3, 2):
        for side in range(2):
            four[side, k].wait_recv()
            last.append(mirror(side, 4 - k))
    for cp in last:
        cp.wait_recv()
    for c in range(2 * nx):
        out[:, :, c * wide:(c + 1) * wide] = yb[c]
    for cp in sends:
        cp.wait_send()


def solution(mesh):
    cache_spec = P('rep', 'seq', 'head', None)

    def local_step(tokens, w_query, w_key, w_value, w_out, k_cache, v_cache, positions):
        batch, shard, kv, dim = k_cache.shape
        model = tokens.shape[1]
        groups = w_query.shape[1] // w_key.shape[1]
        heads = kv * groups
        rows = shard * kv
        flat = (batch, rows, dim)
        anyspec = pl.BlockSpec(memory_space=pl.ANY)
        vspec = pl.BlockSpec(memory_space=pltpu.VMEM)
        steps = batch // NB
        dma = pltpu.SemaphoreType.DMA
        k_new, v_new, acc, stat = pl.pallas_call(
            functools.partial(attend, groups),
            out_shape=(jax.ShapeDtypeStruct(flat, BF16), jax.ShapeDtypeStruct(flat, BF16),
                       jax.ShapeDtypeStruct((heads, batch, dim), F32), jax.ShapeDtypeStruct((PAD, dim), F32)),
            in_specs=[vspec, anyspec, anyspec, anyspec, anyspec, anyspec, pl.BlockSpec(memory_space=pltpu.SMEM)],
            out_specs=(anyspec, anyspec, vspec, vspec),
            scratch_shapes=[
                pltpu.VMEM((groups + 2, model, kv * dim), BF16),
                pltpu.VMEM(flat, BF16),
                pltpu.VMEM(flat, BF16),
                pltpu.VMEM((groups + 2, batch, kv * dim), F32),
                pltpu.VMEM((batch * PAD, dim), F32),
                pltpu.VMEM((batch * PAD, dim), F32),
                dma((groups + 2,)), dma((steps,)), dma((steps,)), dma((steps,)), dma((steps,)),
            ],
            compiler_params=pltpu.CompilerParams(vmem_limit_bytes=56 << 20),
            name='attend',
        )(tokens, w_query, w_key, w_value, k_cache.reshape(flat), v_cache.reshape(flat), positions)

        wide = model // 8
        half = batch // 2
        ns = lax.axis_size('seq')
        y = pl.pallas_call(
            finish,
            out_shape=jax.ShapeDtypeStruct((8, 8, model), BF16),
            in_specs=[vspec, vspec, anyspec],
            out_specs=vspec,
            scratch_shapes=[
                pltpu.VMEM((2 * dim, model), BF16),
                pltpu.VMEM((ns, 2, batch, dim), F32),
                pltpu.VMEM((ns, PAD, dim), F32),
                pltpu.VMEM((dim, dim), F32),
                pltpu.VMEM((batch, 2 * dim), BF16),
                pltpu.VMEM((8, 2, half, wide), F32),
                pltpu.VMEM((8, half, wide), F32),
                pltpu.VMEM((8, half, wide), F32),
                pltpu.VMEM((8, half, wide), F32),
                pltpu.VMEM((2, 4, 8, wide), F32),
                pltpu.VMEM((8, 8, wide), F32),
                pltpu.VMEM((8, 8, 8, wide), BF16),
                dma,
            ] + [dma((8,))] * 16,
            compiler_params=pltpu.CompilerParams(collective_id=0, has_side_effects=True, vmem_limit_bytes=32 << 20),
            name='finish',
        )(acc, stat, w_out)
        return y.reshape(batch, model), k_new.reshape(k_cache.shape), v_new.reshape(v_cache.shape)

    return jax.shard_map(
        local_step,
        mesh=mesh,
        in_specs=(P('rep', None), P(), P(), P(), P(('head', 'seq'), None), cache_spec, cache_spec, P('rep')),
        out_specs=(P('rep', None), cache_spec, cache_spec),
        check_vma=False,
    )
```

time: 207 us -> 75.9 us (0.37)
  blocking collectives: 102 us -> 0 us
  Pallas kernels: 0 us -> 72.5 us
  waiting for transfers between devices: 32.2 us -> 0 us
  other arithmetic: 28.3 us -> 0 us
  matrix products: 25.3 us -> 0 us
  between operations: 14.2 us -> 0.67 us
    psum x2 -> x0, blocking collectives: 76.9 us -> none  [the longest x1 51.9 us: local_step(): y_total = lax.psum(y_part, ('head', 'seq'))]
    pallas_call x0 -> x2, Pallas kernels: none -> 72.5 us  [the longest x1 39.3 us: local_step(): pl.pallas_call(finish, out_shape=jax.ShapeDtypeStruct((8, 8, model), BF16...]
    psum x1 -> x0, waiting for transfers between devices: 32.1 us -> none  [local_step(): lax.psum((local_sum * rescale, local_mix * rescale[..., None]), 'seq')]
    select_n x2 -> x0, other arithmetic: 25.7 us -> none  [the longest x1 25.6 us: local_step(): k_new = jnp.where(is_slot, new_key, k_cache)]
    dot_general x6 -> x0, matrix products: 25.3 us -> none  [the longest x1 9.95 us: local_step(): jnp.dot(tokens, wq_local, preferred_element_type=jnp.float32)]
    pmax x1 -> x0, blocking collectives: 25.1 us -> none  [local_step(): global_max = lax.pmax(local_max, 'seq')]
  transfers between devices with their start and end apart: 1 -> 0, of which waited for: 1 -> 0; matrix products, arithmetic and copies ran while one was open for 0% -> 0% of each run, Pallas kernels for 0% -> 0%
where the time goes in v1:
time: 75.9 us; the launch traced here: 75.8 us
  Pallas kernels  72.5 us (96%)
  local copies, waits for them, and re-layouts  2.57 us (3%)
    pallas_call x1, Pallas kernels, local_step(): pl.pallas_call(finish, out_shape=jax.ShapeDtypeStruct((8, 8, model), BF16...  39.3 us
    pallas_call x1, Pallas kernels, local_step(): pl.pallas_call(functools.partial(attend, groups), out_shape=(jax.ShapeDty...  33.2 us
    unnamed x7, local copies, waits for them, and re-layouts  2.57 us

profile of v1, /device:TPU:97, one launch (start us, length us, event | category | flops | bytes accessed | tf_op | source)
XLA Modules:
  0.0 75.8 jit_solution(9598711629089474568)
XLA Ops:
  0.6 0.0 copy-start
  0.6 33.2 %attend.1 = (bf16[64,512,128]{2,1,0:T(8,128)(2,1)}, bf16[64,512,128]{2,1,0:T(8,128)(2,1)}, f32[12,64,128]{2,1,0:T(8,128)}, f32[16,128]{1,0:T(8,128)}) custom-call(bf16[64,6144]{1,0:T(8,128)(2,1)} %tok.1, bf16[6144,6144]{1,0:T(8,128)(2,1)} %wq.1, bf16[6144,1024]{1,0:T(8,128)(2,1)} %wk.1, bf16[6144,1024]{1,0:T(8,128)(2,1)} %wv.1, ...), custom_call_target="tpu_custom_call" | custom-call | tf_op jit(solution)/shard_map/attend/pallas_call | solution.py:298
  33.8 0.0 copy-done
  33.9 0.0 copy-start.1
  33.9 1.0 %copy-done.1 = f32[12,64,128]{2,1,0:T(8,128)S(1)} copy-done((f32[12,64,128]{2,1,0:T(8,128)S(1)}, f32[12,64,128]{2,1,0:T(8,128)}, u32[]{:S(2)}) %copy-start.1) | copy-done | bytes 393240
  34.9 0.0 copy-start.2
  34.9 0.7 copy-done.2
  35.6 39.3 %finish.1 = bf16[8,8,6144]{2,1,0:T(8,128)(2,1)S(1)} custom-call(f32[12,64,128]{2,1,0:T(8,128)S(1)} %copy-done.1, f32[16,128]{1,0:T(8,128)S(1)} %copy-done.2, bf16[192,6144]{1,0:T(8,128)(2,1)S(1)} %copy-done), custom_call_target="tpu_custom_call" | custom-call | tf_op jit(solution)/shard_map/finish/pallas_call | solution.py:320
  74.9 0.9 %copy.12 = bf16[64,6144]{1,0:T(8,128)(2,1)} copy(bf16[64,6144]{1,0:T(8,128)(2,1)S(1)} %bitcast.5) | data formatting | bytes 1572864
Async XLA Ops:
  0.6 33.2 %copy-start = (bf16[192,6144]{1,0:T(8,128)(2,1)S(1)}, bf16[192,6144]{1,0:T(8,128)(2,1)}, u32[]{:S(2)}) copy-start(bf16[192,6144]{1,0:T(8,128)(2,1)} %wo.1) | copy-start | bytes 7077892
  33.9 1.0 %copy-start.1 = (f32[12,64,128]{2,1,0:T(8,128)S(1)}, f32[12,64,128]{2,1,0:T(8,128)}, u32[]{:S(2)}) copy-start(f32[12,64,128]{2,1,0:T(8,128)} %get-tuple-element.7.acch) | copy-start | bytes 1179652
  34.9 0.7 copy-start.2

commit v2 on v1

--- a/solution.py
+++ b/solution.py
@@ -11,97 +11,134 @@
 BF16 = jnp.bfloat16
 F32 = jnp.float32
 PAD = 16
-NB = 8
-
-
-def attend(groups, tok, wq, wk, wv, kc, vc, pos, ko, vo, acch, stat,
-           wbuf, kb, vb, pj, q2, accs, wsem, ksem, vsem, kosem, vosem):
+NB = 16
+
+
+def project(groups, tokens, wq, wk, wv, kc, vc, pj, kb, vb, tok, wbuf, tsem, wsem, ssem, rsem, ksem, vsem):
     head = lax.axis_index('head')
+    s = lax.axis_index('seq')
+    p = lax.rem(s, 2)
+    width = pj.shape[-1]
+    per = wbuf.shape[0]
+    partner = {'head': head, 'seq': s + 1 - 2 * p}
+
+    def load(i, src, block):
+        return pltpu.make_async_copy(src.at[:, pl.ds(pl.multiple_of(block * width, width), width)], wbuf.at[i], wsem.at[i])
+
+    first = pltpu.make_async_copy(tokens, tok, tsem)
+    first.start()
+    for i in range(per):
+        @pl.when(p == 0)
+        def _():
+            load(i, wq, head * groups + i).start()
+
+        @pl.when(p == 1)
+        def _():
+            if per + i < groups:
+                load(i, wq, head * groups + per + i).start()
+            else:
+                load(i, wk if per + i == groups else wv, head).start()
+
+    caches = [pltpu.make_async_copy(kc, kb, ksem), pltpu.make_async_copy(vc, vb, vsem)]
+    for cp in caches:
+        cp.start()
+    barrier = pltpu.get_barrier_semaphore()
+    pl.semaphore_signal(barrier, inc=1, device_id=partner, device_id_type=MESH)
+    pl.semaphore_wait(barrier, 1)
+    sends = []
+    first.wait()
+    for i in range(per):
+        load(i, wq, 0).wait()
+        slot = p * per + i
+        pj[slot] = jnp.dot(tok[...], wbuf[i], preferred_element_type=F32).astype(BF16)
+        cp = pltpu.make_async_remote_copy(src_ref=pj.at[slot], dst_ref=pj.at[slot], send_sem=ssem.at[i],
+                                          recv_sem=rsem.at[i], device_id=partner, device_id_type=MESH)
+        cp.start()
+        sends.append(cp)
+    for cp in sends:
+        cp.wait_recv()
+    for cp in sends:
+        cp.wait_send()
+    for cp in caches:
+        cp.wait()
+
+
+def attend(groups, pj, kin, vin, pos, ko, vo, kb, vb, acch, stat, q2, nkv, accs, osem):
     seq = lax.axis_index('seq')
-    batch, rows, dim = kc.shape
+    batch, rows, dim = kb.shape
     shard = rows // 2
     heads = 2 * groups
-    nq = groups
-    width = 2 * dim
     steps = batch // NB
-
-    def weight(i):
-        if i < nq:
-            src = wq.at[:, pl.ds(pl.multiple_of((head * nq + i) * width, width), width)]
-        else:
-            src = (wk if i == nq else wv).at[:, pl.ds(pl.multiple_of(head * width, width), width)]
-        return pltpu.make_async_copy(src, wbuf.at[i], wsem.at[i])
-
-    def block(src, dst, sem, c):
-        span = pl.ds(pl.multiple_of(c * NB, NB), NB)
-        return pltpu.make_async_copy(src.at[span], dst.at[span], sem.at[c])
-
-    for i in range(nq + 2):
-        weight(i).start()
-    for c in range(steps):
-        block(kc, kb, ksem, c).start()
-        block(vc, vb, vsem, c).start()
     q2[...] = jnp.zeros_like(q2)
-
-    def project(i, carry):
-        pltpu.make_async_copy(wq.at[:, pl.ds(0, width)], wbuf.at[i], wsem.at[i]).wait()
-        out = jnp.dot(tok[...], wbuf[i], preferred_element_type=F32)
-        pj[i] = out.astype(BF16).astype(F32)
-        return carry
-
-    lax.fori_loop(0, nq + 2, project, 0)
     for h in range(heads):
-        q2[pl.ds(h, batch, stride=PAD), :] = pj[h // 2][:, (h % 2) * dim:(h % 2 + 1) * dim]
+        q2[pl.ds(h, batch, stride=PAD), :] = pj[h // 2][:, (h % 2) * dim:(h % 2 + 1) * dim].astype(F32)
+    nkv[0] = pj[groups].astype(F32)
+    nkv[1] = pj[groups + 1].astype(F32)
 
     row16 = lax.broadcasted_iota(jnp.int32, (16, dim), 0)
     even = (row16 & 1) == 0
-    lane = lax.broadcasted_iota(jnp.int32, (PAD, dim), 1)
-    col = lax.broadcasted_iota(jnp.int32, (PAD, rows), 1)
-    rid = lax.broadcasted_iota(jnp.int32, (PAD, rows), 0)
-    slot = col >> 1
-    own = jnp.where(rid < groups, 0, jnp.where(rid < heads, 1, 2)) == (col & 1)
-    slot = jnp.where(own, slot, jnp.int32(1 << 30))
-
-    def step(c, st):
-        def update(buf, which):
-            for i in range(NB):
-                b = c * NB + i
-                t = pos[b] - seq * shard
-                inside = (t >= 0) & (t < shard)
-                tc = jnp.clip(t, 0, shard - 1)
-                start = pl.multiple_of((tc >> 3) * 16, 16)
-                hit = ((row16 >> 1) == (tc & 7)) & inside
-                new = pj[which, pl.ds(b, 1), :]
+    lanes = NB * PAD
+    lane = lax.broadcasted_iota(jnp.int32, (8, lanes), 1)
+    sub = lax.broadcasted_iota(jnp.int32, (8, lanes), 0)
+    hl = lane & (PAD - 1)
+    match = jnp.where(hl < groups, 0, jnp.where(hl < heads, 1, 2)) == (sub & 1)
+    tile = lax.broadcasted_iota(jnp.int32, (rows // 8, 8, lanes), 0) * 4
+
+    def out(j, c):
+        span = pl.ds(pl.multiple_of(c * NB, NB), NB)
+        src, dst = ((kb, ko), (vb, vo))[j]
+        return pltpu.make_async_copy(src.at[span], dst.at[span], osem.at[j, c])
+
+    def step(c, carry):
+        limit = jnp.zeros((8, lanes), jnp.int32)
+        for i in range(NB):
+            b = c * NB + i
+            t = pos[b] - seq * shard
+            limit = jnp.where(lane // PAD == i, t, limit)
+            inside = (t >= 0) & (t < shard)
+            tc = jnp.clip(t, 0, shard - 1)
+            start = pl.multiple_of((tc >> 3) * 16, 16)
+            hit = ((row16 >> 1) == (tc & 7)) & inside
+            for j, buf in enumerate((kb, vb)):
+                new = nkv[j, pl.ds(b, 1), :]
                 new = jnp.where(even, new[:, :dim], new[:, dim:])
                 old = buf[b, pl.ds(start, 16), :].astype(F32)
                 buf[b, pl.ds(start, 16), :] = jnp.where(hit, new, old).astype(BF16)
-
-        block(kc, kb, ksem, c).wait()
-        update(kb, nq)
-        block(kb, ko, kosem, c).start()
-        block(vc, vb, vsem, c).wait()
-        update(vb, nq + 1)
-        block(vb, vo, vosem, c).start()
-        for i in range(NB):
-            b = c * NB + i
-            t = pos[b] - seq * shard
-            q = q2[pl.ds(pl.multiple_of(b * PAD, PAD), PAD), :].astype(BF16)
-            s = lax.dot_general(q, kb[b], (((1,), (1,)), ((), ())), preferred_element_type=F32)
-            s = jnp.where(slot <= t, s * dim ** -0.5, -jnp.inf)
-            m = jnp.max(s, axis=-1, keepdims=True)
-            w = jnp.exp(s - jnp.where(m == -jnp.inf, 0.0, m))
-            l = jnp.sum(w, axis=-1, keepdims=True)
-            acc = jnp.dot(w.astype(BF16), vb[b], preferred_element_type=F32)
-            accs[pl.ds(pl.multiple_of(b * PAD, PAD), PAD), :] = acc
-            st = jnp.where(lane == b, m, jnp.where(lane == b + batch, l, st))
-        return st
-
-    stat[...] = lax.fori_loop(0, steps, step, jnp.zeros((PAD, dim), F32))
+        out(0, c).start()
+        out(1, c).start()
+        edge = jnp.where(match, limit, -1) - (sub >> 1)
+        qt = jnp.transpose(q2[pl.ds(pl.multiple_of(c * lanes, lanes), lanes), :]).astype(BF16)
+        ql = lax.broadcasted_iota(jnp.int32, (dim, lanes), 1) // PAD
+        s = jnp.zeros((rows, lanes), F32)
+        for j in range(NB // 2):
+            b = c * NB + 2 * j
+            lhs = jnp.concatenate([kb[b], kb[b + 1]], axis=1)
+            zero = jnp.zeros_like(qt)
+            rhs = jnp.concatenate([jnp.where(ql == 2 * j, qt, zero), jnp.where(ql == 2 * j + 1, qt, zero)], axis=0)
+            s = s + jnp.dot(lhs, rhs, preferred_element_type=F32)
+        s = s.reshape(rows // 8, 8, lanes) * dim ** -0.5
+        s = jnp.where(tile <= edge[None], s, -jnp.inf)
+        m = jnp.max(jnp.max(s, axis=0), axis=0, keepdims=True)
+        w = jnp.exp(s - jnp.where(m == -jnp.inf, 0.0, m)[None])
+        l = jnp.sum(jnp.sum(w, axis=0), axis=0, keepdims=True)
+        for r in range(lanes // dim):
+            stat[pl.ds(c * (lanes // dim) + r, 1), :] = m[:, r * dim:(r + 1) * dim]
+            stat[pl.ds(8 + c * (lanes // dim) + r, 1), :] = l[:, r * dim:(r + 1) * dim]
+        wt = jnp.transpose(w.reshape(rows, lanes)).astype(BF16)
+        for j in range(NB // 2):
+            b = c * NB + 2 * j
+            rhs = jnp.concatenate([vb[b], vb[b + 1]], axis=1)
+            a = jnp.dot(wt[2 * PAD * j:2 * PAD * (j + 1)], rhs, preferred_element_type=F32)
+            accs[pl.ds(pl.multiple_of(b * PAD, PAD), PAD), :] = a[:PAD, :dim]
+            accs[pl.ds(pl.multiple_of(b * PAD + PAD, PAD), PAD), :] = a[PAD:, dim:]
+        return carry
+
+    lax.fori_loop(0, steps, step, 0)
     for h in range(heads):
         acch[h] = accs[pl.ds(h, batch, stride=PAD), :]
     for c in range(steps):
-        block(kb, ko, kosem, c).wait()
-        block(vb, vo, vosem, c).wait()
+        out(0, c).wait()
+        out(1, c).wait()
 
 
 def finish(acch, stat, wo, out, wob, rx, srx, fs, lhs, yp, dx, z, r1, s1, r2, yb,
@@ -165,18 +202,24 @@
         cp.wait_recv()
 
     h0 = first(s)
-    tiles = [srx[i, pl.ds(h0, 2), :] for i in range(ns)]
-    top = functools.reduce(jnp.maximum, tiles)
-    scale = [jnp.exp(t - top) for t in tiles]
-    total = functools.reduce(lambda a, b: a + b, [e * pltpu.roll(t, dim // 2, 1) for e, t in zip(scale, tiles)])
+    rows = batch // 8
+    peaks = [srx[i, :rows] for i in range(ns)]
+    top = functools.reduce(jnp.maximum, peaks)
+    scale = [jnp.exp(m - top) for m in peaks]
+    total = functools.reduce(lambda a, b: a + b, [e * srx[i, rows:] for i, e in enumerate(scale)])
     for i in range(ns):
-        fs[2 * i:2 * i + 2, :] = scale[i] / total
-    ft = jnp.transpose(fs[...])[:batch]
+        fs[i * rows:(i + 1) * rows, :] = scale[i] / total
+    fs[...] = jnp.transpose(fs[...])
     lane = lax.broadcasted_iota(jnp.int32, (batch, dim), 1)
     for j in range(2):
-        acc = ft[:, j:j + 1] * acch[h0 + j]
-        for i in range(1, ns):
-            acc = acc + ft[:, 2 * i + j:2 * i + j + 1] * rx[i, j]
+        col = fs[pl.ds(h0 + j, 8, stride=PAD), :]
+        parts = []
+        for c in range(rows):
+            acc = col[:, c:c + 1] * acch[h0 + j, 8 * c:8 * c + 8]
+            for i in range(1, ns):
+                acc = acc + col[:, i * rows + c:i * rows + c + 1] * rx[i, j, 8 * c:8 * c + 8]
+            parts.append(acc)
+        acc = jnp.concatenate(parts, axis=0)
         keep = (lane >= dim // 2) if j == 0 else (lane < dim // 2)
         keep = keep | (p == j)
         lhs[:, j * dim:(j + 1) * dim] = jnp.where(keep, acc, 0.0).astype(BF16)
@@ -291,28 +334,37 @@
         heads = kv * groups
         rows = shard * kv
         flat = (batch, rows, dim)
+        hspec = pl.BlockSpec(memory_space=pltpu.HBM)
         anyspec = pl.BlockSpec(memory_space=pl.ANY)
         vspec = pl.BlockSpec(memory_space=pltpu.VMEM)
-        steps = batch // NB
         dma = pltpu.SemaphoreType.DMA
-        k_new, v_new, acc, stat = pl.pallas_call(
+        cache = jax.ShapeDtypeStruct(flat, BF16)
+        blocks = groups + 2
+        per = blocks // 2
+        proj, kb, vb = pl.pallas_call(
+            functools.partial(project, groups),
+            out_shape=(jax.ShapeDtypeStruct((blocks, batch, kv * dim), BF16), cache, cache),
+            in_specs=[hspec] * 6,
+            out_specs=(vspec,) * 3,
+            scratch_shapes=[pltpu.VMEM(tokens.shape, BF16), pltpu.VMEM((per, model, kv * dim), BF16), dma,
+                            dma((per,)), dma((per,)), dma((per,)), dma, dma],
+            compiler_params=pltpu.CompilerParams(collective_id=1, has_side_effects=True, vmem_limit_bytes=34 << 20),
+            cost_estimate=pl.CostEstimate(flops=10**10, bytes_accessed=30 * 10**6, transcendentals=0),
+            name='project',
+        )(tokens, w_query, w_key, w_value, k_cache.reshape(flat), v_cache.reshape(flat))
+        k_new, v_new, _, _, acc, stat = pl.pallas_call(
             functools.partial(attend, groups),
-            out_shape=(jax.ShapeDtypeStruct(flat, BF16), jax.ShapeDtypeStruct(flat, BF16),
-                       jax.ShapeDtypeStruct((heads, batch, dim), F32), jax.ShapeDtypeStruct((PAD, dim), F32)),
-            in_specs=[vspec, anyspec, anyspec, anyspec, anyspec, anyspec, pl.BlockSpec(memory_space=pltpu.SMEM)],
-            out_specs=(anyspec, anyspec, vspec, vspec),
-            scratch_shapes=[
-                pltpu.VMEM((groups + 2, model, kv * dim), BF16),
-                pltpu.VMEM(flat, BF16),
-                pltpu.VMEM(flat, BF16),
-                pltpu.VMEM((groups + 2, batch, kv * dim), F32),
-                pltpu.VMEM((batch * PAD, dim), F32),
-                pltpu.VMEM((batch * PAD, dim), F32),
-                dma((groups + 2,)), dma((steps,)), dma((steps,)), dma((steps,)), dma((steps,)),
-            ],
-            compiler_params=pltpu.CompilerParams(vmem_limit_bytes=56 << 20),
+            out_shape=(cache, cache, cache, cache, jax.ShapeDtypeStruct((heads, batch, dim), F32),
+                       jax.ShapeDtypeStruct((PAD, dim), F32)),
+            in_specs=[vspec, vspec, vspec, pl.BlockSpec(memory_space=pltpu.SMEM)],
+            out_specs=(hspec, hspec, vspec, vspec, vspec, vspec),
+            input_output_aliases={1: 2, 2: 3},
+            scratch_shapes=[pltpu.VMEM((batch * PAD, dim), F32), pltpu.VMEM((2, batch, kv * dim), F32),
+                            pltpu.VMEM((batch * PAD, dim), F32), dma((2, batch // NB))],
+            compiler_params=pltpu.CompilerParams(vmem_limit_bytes=24 << 20),
+            cost_estimate=pl.CostEstimate(flops=10**10, bytes_accessed=17 * 10**6, transcendentals=0),
             name='attend',
-        )(tokens, w_query, w_key, w_value, k_cache.reshape(flat), v_cache.reshape(flat), positions)
+        )(proj, kb, vb, positions)
 
         wide = model // 8
         half = batch // 2

time: 75.9 us -> 61.2 us (0.81)
  Pallas kernels: 72.5 us -> 58.4 us
    pallas_call x1 -> x2, Pallas kernels: 33.2 us -> 19 us  [the longest x1 9.68 us: local_step(): pl.pallas_call(functools.partial(project, groups), out_shape=(jax.ShapeDt...]
where the time goes in v2:
time: 61.2 us; the launch traced here: 61.1 us
  Pallas kernels  58.4 us (95%)
  local copies, waits for them, and re-layouts  2.02 us (3%)
  between operations  0.69 us (1%)
    pallas_call x1, Pallas kernels, local_step(): pl.pallas_call(finish, out_shape=jax.ShapeDtypeStruct((8, 8, model), BF16...  39.4 us
    pallas_call x1, Pallas kernels, local_step(): pl.pallas_call(functools.partial(project, groups), out_shape=(jax.ShapeDt...  9.68 us
    pallas_call x1, Pallas kernels, local_step(): pl.pallas_call(functools.partial(attend, groups), out_shape=(cache, cache...  9.37 us
    unnamed x7, local copies, waits for them, and re-layouts  2.02 us

profile of v2, /device:TPU:97, one launch (start us, length us, event | category | flops | bytes accessed | tf_op | source)
XLA Modules:
  0.0 61.1 jit_solution(5835083191034570350)
XLA Ops:
  0.6 0.0 copy-start.1
  0.6 1.1 %copy-done.1 = bf16[64,6144]{1,0:T(8,128)(2,1)S(1)} copy-done((bf16[64,6144]{1,0:T(8,128)(2,1)S(1)}, bf16[64,6144]{1,0:T(8,128)(2,1)}, u32[]{:S(2)}) %copy-start.1) | copy-done | bytes 786456
  1.8 0.0 copy-start.2
  1.8 9.7 %project.1 = (bf16[8,64,256]{2,1,0:T(8,128)(2,1)S(1)}, bf16[64,512,128]{2,1,0:T(8,128)(2,1)S(1)}, bf16[64,512,128]{2,1,0:T(8,128)(2,1)S(1)}) custom-call(bf16[64,6144]{1,0:T(8,128)(2,1)S(1)} %copy-done.1, bf16[6144,6144]{1,0:T(8,128)(2,1)} %wq.1, bf16[6144,1024]{1,0:T(8,128)(2,1)} %wk.1, bf16[6144,1024]{1,0:T(8,128)(2,1)} %wv.1, ...), custom_call_target="tpu_custom_call" | custom-call | flops 10000000000 | bytes 30000000 | tf_op jit(solution)/shard_map/project/pallas_call | solution.py:344
  11.5 0.0 copy-done.2
  11.5 0.0 copy-start
  11.5 9.4 %attend.1 = (bf16[64,512,128]{2,1,0:T(8,128)(2,1)}, bf16[64,512,128]{2,1,0:T(8,128)(2,1)}, bf16[64,512,128]{2,1,0:T(8,128)(2,1)S(1)}, bf16[64,512,128]{2,1,0:T(8...) custom-call(bf16[8,64,256]{2,1,0:T(8,128)(2,1)S(1)} %get-tuple-eleme, ...), custom_call_target="tpu_custom_call", output_to_operand_aliasing={{2}: (1, {}), {3}: (2, {})} | custom-call | flops 10000000000 | bytes 17000000 | tf_op jit(solution)/shard_map/attend/pallas_call | solution.py:355
  20.9 0.0 copy-done
  20.9 39.4 %finish.1 = bf16[8,8,6144]{2,1,0:T(8,128)(2,1)S(1)} custom-call(f32[12,64,128]{2,1,0:T(8,128)S(1)} %get-tuple-element.13.acch, f32[16,128]{1,0:T(8,128)S(1)} %get-tuple-element.14.stat, bf16[192,6144]{1,0:T(8,128)(2,1)S(1)} %copy-done), custom_call_target="tpu_custom_call" | custom-call | tf_op jit(solution)/shard_map/finish/pallas_call | solution.py:372
  60.2 0.9 %copy.16 = bf16[64,6144]{1,0:T(8,128)(2,1)} copy(bf16[64,6144]{1,0:T(8,128)(2,1)S(1)} %bitcast.5) | data formatting | bytes 1572864
Async XLA Ops:
  0.6 1.1 %copy-start.1 = (bf16[64,6144]{1,0:T(8,128)(2,1)S(1)}, bf16[64,6144]{1,0:T(8,128)(2,1)}, u32[]{:S(2)}) copy-start(bf16[64,6144]{1,0:T(8,128)(2,1)} %tokens.1) | copy-start | bytes 2359300
  1.8 9.7 %copy-start.2 = (s32[64]{0:T(128)S(1)}, s32[64]{0:T(128)}, u32[]{:S(2)}) copy-start(s32[64]{0:T(128)} %pos.1) | copy-start | bytes 772
  11.5 9.4 %copy-start = (bf16[192,6144]{1,0:T(8,128)(2,1)S(1)}, bf16[192,6144]{1,0:T(8,128)(2,1)}, u32[]{:S(2)}) copy-start(bf16[192,6144]{1,0:T(8,128)(2,1)} %wo.1) | copy-start | bytes 7077892

commit v3 on v2

v3 whole, which is shorter than its diff:
```python
import functools

import jax
import jax.numpy as jnp
from jax import lax
from jax.experimental import pallas as pl
from jax.experimental.pallas import tpu as pltpu
from jax.sharding import PartitionSpec as P

MESH = pl.DeviceIdType.MESH
BF16 = jnp.bfloat16
F32 = jnp.float32
PAD = 16
NB = 16
NC = 2


def project(groups, tokens, wq, wk, wv, kc, vc, pj, kb, vb, tok, wbuf, tsem, wsem, ssem, rsem, ksem, vsem):
    head = lax.axis_index('head')
    s = lax.axis_index('seq')
    ns = lax.axis_size('seq')
    parts, depth, width = wbuf.shape

    def load(i, src, block):
        rows = pl.ds(i * depth, depth)
        return pltpu.make_async_copy(src.at[rows, pl.ds(pl.multiple_of(block * width, width), width)], wbuf.at[i], wsem.at[i])

    first = pltpu.make_async_copy(tokens, tok, tsem)
    first.start()
    for i in range(parts):
        @pl.when(s < groups)
        def _():
            load(i, wq, head * groups + s).start()

        @pl.when(s == groups)
        def _():
            load(i, wk, head).start()

        @pl.when(s == groups + 1)
        def _():
            load(i, wv, head).start()

    caches = [pltpu.make_async_copy(kc, kb, ksem), pltpu.make_async_copy(vc, vb, vsem)]
    for cp in caches:
        cp.start()
    barrier = pltpu.get_barrier_semaphore()
    for k in range(1, ns):
        pl.semaphore_signal(barrier, inc=1, device_id={'head': head, 'seq': lax.rem(s + k, ns)}, device_id_type=MESH)
    first.wait()
    acc = jnp.zeros((tok.shape[0], width), F32)
    for i in range(parts):
        load(i, wq, 0).wait()
        acc = acc + jnp.dot(tok[:, i * depth:(i + 1) * depth], wbuf[i], preferred_element_type=F32)
    pj[s] = acc.astype(BF16)
    pl.semaphore_wait(barrier, ns - 1)
    sends = []
    for k in (4, 5, 3, 2, 6, 7, 1):
        cp = pltpu.make_async_remote_copy(src_ref=pj.at[s], dst_ref=pj.at[s], send_sem=ssem.at[k], recv_sem=rsem.at[k],
                                          device_id={'head': head, 'seq': lax.rem(s + k, ns)}, device_id_type=MESH)
        cp.start()
        sends.append(cp)
    for cp in sends:
        cp.wait_recv()
    for cp in sends:
        cp.wait_send()
    for cp in caches:
        cp.wait()


def attend(groups, pj, kin, vin, pos, ko, vo, kb, vb, acch, stat, q2, nkv, accs, sb, osem):
    seq = lax.axis_index('seq')
    batch, rows, dim = kb.shape
    shard = rows // 2
    heads = 2 * groups
    steps = batch // NB
    q2[...] = jnp.zeros_like(q2)
    for h in range(heads):
        q2[pl.ds(h, batch, stride=PAD), :] = pj[h // 2][:, (h % 2) * dim:(h % 2 + 1) * dim].astype(F32)
    nkv[0] = pj[groups].astype(F32)
    nkv[1] = pj[groups + 1].astype(F32)

    row16 = lax.broadcasted_iota(jnp.int32, (16, dim), 0)
    even = (row16 & 1) == 0
    lanes = NB * PAD
    lane = lax.broadcasted_iota(jnp.int32, (8, lanes), 1)
    sub = lax.broadcasted_iota(jnp.int32, (8, lanes), 0)
    hl = lane & (PAD - 1)
    match = jnp.where(hl < groups, 0, jnp.where(hl < heads, 1, 2)) == (sub & 1)
    tile = lax.broadcasted_iota(jnp.int32, (rows // 8, 8, lanes), 0) * 4

    def out(j, c):
        span = pl.ds(pl.multiple_of(c * NB, NB), NB)
        src, dst = ((kb, ko), (vb, vo))[j]
        return pltpu.make_async_copy(src.at[span], dst.at[span], osem.at[j, c])

    def refresh(c, carry):
        fresh = []
        for i in range(NB):
            b = c * NB + i
            t = pos[b] - seq * shard
            inside = (t >= 0) & (t < shard)
            tc = jnp.clip(t, 0, shard - 1)
            start = pl.multiple_of((tc >> 3) * 16, 16)
            hit = ((row16 >> 1) == (tc & 7)) & inside
            for j, buf in enumerate((kb, vb)):
                new = nkv[j, pl.ds(b, 1), :]
                new = jnp.where(even, new[:, :dim], new[:, dim:])
                old = buf[b, pl.ds(start, 16), :].astype(F32)
                fresh.append((buf, b, start, jnp.where(hit, new, old).astype(BF16)))
        for buf, b, start, value in fresh:
            buf[b, pl.ds(start, 16), :] = value
        out(0, c).start()
        out(1, c).start()
        return carry

    lax.fori_loop(0, steps, refresh, 0)
    ql = lax.broadcasted_iota(jnp.int32, (dim, lanes), 1) // PAD

    def scores(c):
        qt = jnp.transpose(q2[c * lanes:(c + 1) * lanes, :]).astype(BF16)
        zero = jnp.zeros_like(qt)
        s = jnp.zeros((rows, lanes), F32)
        for j in range(NB // 2):
            b = c * NB + 2 * j
            lhs = jnp.concatenate([kb[b], kb[b + 1]], axis=1)
            rhs = jnp.concatenate([jnp.where(ql == 2 * j, qt, zero), jnp.where(ql == 2 * j + 1, qt, zero)], axis=0)
            s = s + jnp.dot(lhs, rhs, preferred_element_type=F32)
        sb[c % 2] = s

    def mix(c):
        limit = jnp.zeros((8, lanes), jnp.int32)
        for i in range(NB):
            limit = jnp.where(lane // PAD == i, pos[c * NB + i] - seq * shard, limit)
        edge = jnp.where(match, limit, -1) - (sub >> 1)
        s = sb[c % 2].reshape(rows // 8, 8, lanes) * dim ** -0.5
        s = jnp.where(tile <= edge[None], s, -jnp.inf)
        m = jnp.max(jnp.max(s, axis=0), axis=0, keepdims=True)
        w = jnp.exp(s - jnp.where(m == -jnp.inf, 0.0, m)[None])
        l = jnp.sum(jnp.sum(w, axis=0), axis=0, keepdims=True)
        for r in range(lanes // dim):
            g = c * (lanes // dim) + r
            g = g // 4 * 8 + g % 4
            stat[g:g + 1, :] = m[:, r * dim:(r + 1) * dim]
            stat[g + 4:g + 5, :] = l[:, r * dim:(r + 1) * dim]
        wt = jnp.transpose(w.reshape(rows, lanes).astype(BF16))
        for j in range(NB // 2):
            b = c * NB + 2 * j
            rhs = jnp.concatenate([vb[b], vb[b + 1]], axis=1)
            a = jnp.dot(wt[2 * PAD * j:2 * PAD * (j + 1)], rhs, preferred_element_type=F32)
            accs[b * PAD:(b + 1) * PAD, :] = a[:PAD, :dim]
            accs[(b + 1) * PAD:(b + 2) * PAD, :] = a[PAD:, dim:]

    scores(0)
    for c in range(steps):
        if c + 1 < steps:
            scores(c + 1)
        mix(c)
    for h in range(heads):
        acch[h] = accs[pl.ds(h, batch, stride=PAD), :]
    for c in range(steps):
        out(0, c).wait()
        out(1, c).wait()


def finish(acch, stat, wo, out, wob, rx, srx, fs, lhs, z, r1, s1, r2, yb,
           osem, w_s, w_r, d_s, d_r, t_s, t_r, a_s, a_r, b_s, b_r, c_s, c_r, e_s, e_r, f_s, f_r):
    y = lax.axis_index('head')
    s = lax.axis_index('seq')
    ny = lax.axis_size('head')
    ns = lax.axis_size('seq')
    nx = ns // 2
    x = s // 2
    p = lax.rem(s, 2)
    heads, batch, dim = acch.shape
    wrows = wo.shape[0]
    nc, per, step = rx.shape[1:4]
    half = nc * step
    wide = z.shape[-1]
    short = wide // 2

    def on_x(k):
        return {'head': y, 'seq': lax.rem(x + k, nx) * 2 + p}

    def on_y(k):
        return {'head': lax.rem(y + k, ny), 'seq': s}

    def copy(src, dst, send, recv, dev):
        return pltpu.make_async_remote_copy(src_ref=src, dst_ref=dst, send_sem=send, recv_sem=recv,
                                            device_id=dev, device_id_type=MESH)

    partner = {'head': y, 'seq': x * 2 + 1 - p}
    mine = wob.at[pl.ds(pl.multiple_of(p * wrows, wrows), wrows), :]
    load = pltpu.make_async_copy(wo, mine, osem)
    load.start()

    barrier = pltpu.get_barrier_semaphore()
    for k in range(1, ns):
        pl.semaphore_signal(barrier, inc=1, device_id={'head': y, 'seq': lax.rem(s + k, ns)}, device_id_type=MESH)
    for k in range(1, ny):
        pl.semaphore_signal(barrier, inc=1, device_id=on_y(k), device_id_type=MESH)
    pl.semaphore_wait(barrier, ns - 1 + ny - 1)

    sends = []

    def go(*a):
        cp = copy(*a)
        cp.start()
        sends.append(cp)
        return cp

    stats, parts = [], {c: [] for c in range(nc)}
    for c in range(nc):
        for k in (4, 5, 3, 2, 6, 7, 1):
            dest = lax.rem(s + k, ns)
            dev = {'head': y, 'seq': dest}
            side = lax.rem(dest, 2)
            if c == 0:
                rows = pl.ds(pl.multiple_of(side * 8, 8), 8)
                stats.append(go(stat.at[rows], srx.at[k], t_s.at[k], t_r.at[k], dev))
            rows = pl.ds(pl.multiple_of(side * half + c * step, step), step)
            parts[c].append(go(acch.at[pl.ds((dest // 2) * per, per), rows], rx.at[k, c], d_s.at[c, k], d_r.at[c, k], dev))
    wcopy = go(wo, mine, w_s, w_r, partner)
    srx[0] = stat[pl.ds(pl.multiple_of(p * 8, 8), 8)]
    fs[...] = jnp.zeros_like(fs)
    for cp in stats:
        cp.wait_recv()
    n8 = half // 8
    top = functools.reduce(jnp.maximum, [srx[i, :n8] for i in range(ns)])
    scale = [jnp.exp(srx[i, :n8] - top) for i in range(ns)]
    total = functools.reduce(lambda a, b: a + b, [e * srx[i, n8:] for i, e in enumerate(scale)])
    for i in range(ns):
        fs[i * n8:(i + 1) * n8, :] = scale[i] / total
    fs[...] = jnp.transpose(fs[...])

    def block_of(side, k):
        return lax.rem(x + k, nx) if side == 0 else nx + lax.rem(y + k, ny)

    def near(side, k):
        return on_x(k) if side == 0 else on_y(k)

    def far(side, k):
        return on_y(k) if side == 0 else on_x(k)

    def order_of(side):
        return y if side == 0 else x

    cols = [fs[pl.ds(x * per + j, 8, stride=PAD), :] for j in range(per)]
    one, two, three, four, last = {}, {}, {}, {}, {c: [] for c in range(nc)}
    for c in range(nc):
        for cp in parts[c]:
            cp.wait_recv()
        for j in range(per):
            rows = []
            for g in range(step // 8):
                lead = c * (step // 8) + g
                acc = cols[j][:, lead:lead + 1] * acch[x * per + j, pl.ds(half * p + 8 * lead, 8)]
                for i in range(1, ns):
                    acc = acc + cols[j][:, i * n8 + lead:i * n8 + lead + 1] * rx[i, c, j, 8 * g:8 * g + 8]
                rows.append(acc)
            lhs[c, :, j * dim:(j + 1) * dim] = jnp.concatenate(rows, axis=0).astype(BF16)
        if c == 0:
            load.wait()
            wcopy.wait_recv()
        for k in (2, 1, 3, 0):
            for side in range(2):
                n = block_of(side, k)
                z[c, side * 4 + k] = jnp.dot(lhs[c], wob[:, pl.ds(pl.multiple_of(n * wide, wide), wide)],
                                             preferred_element_type=F32)
            for side in range(2 if k else 0):
                i = side * 4 + k
                one[c, side, k] = go(z.at[c, i], r1.at[c, i], a_s.at[c, i], a_r.at[c, i], near(side, k))

    for c in range(nc):
        for side in range(2):
            base = side * 4
            for k in (1, 3, 2):
                one[c, side, k].wait_recv()
            v = z[c, base] + r1[c, base + 1] + r1[c, base + 2] + r1[c, base + 3]
            for r in range(4):
                s1[c, side, r] = v[8 * (r // 2):8 * (r // 2) + 8, short * (r % 2):short * (r % 2 + 1)]
            for k in (2, 1, 3):
                dest = lax.rem(order_of(side) + k, 4)
                i = base + k
                two[c, side, k] = go(s1.at[c, side, dest], r2.at[c, i], b_s.at[c, i], b_r.at[c, i], far(side, k))

    for c in range(nc):
        for side in range(2):
            base = side * 4
            for k in (1, 3, 2):
                two[c, side, k].wait_recv()
            v = s1[c, side, order_of(side)] + r2[c, base + 1] + r2[c, base + 2] + r2[c, base + 3]
            part = yb.at[block_of(side, 0), p, c, order_of(side)]
            part[...] = v.astype(BF16)
            for k in (2, 1, 3):
                i = base + k
                three[c, side, k] = go(part, part, c_s.at[c, i], c_r.at[c, i], far(side, k))

    def mirror(c, side, k):
        part = yb.at[block_of(side, 4 - k), p, c]
        i = side * 4 + k
        last[c].append(go(part, part, f_s.at[c, i], f_r.at[c, i], partner))

    for c in range(nc):
        for side in range(2):
            part = yb.at[block_of(side, 0), p, c]
            for k in (1, 3, 2):
                three[c, side, k].wait_recv()
            for k in (2, 1, 3):
                i = side * 4 + k
                four[c, side, k] = go(part, part, e_s.at[c, i], e_r.at[c, i], near(side, k))
            mirror(c, side, 0)
    for c in range(nc):
        for k in (1, 3, 2):
            for side in range(2):
                four[c, side, k].wait_recv()
                mirror(c, side, k)
    for c in range(nc):
        for cp in last[c]:
            cp.wait_recv()
        for n in range(2 * nx):
            for q in range(2):
                for r in range(4):
                    row = q * 4 + c * 2 + r // 2
                    left = n * wide + (r % 2) * short
                    out[row, :, left:left + short] = yb[n, q, c, r]
    for cp in sends:
        cp.wait_send()


def solution(mesh):
    cache_spec = P('rep', 'seq', 'head', None)

    def local_step(tokens, w_query, w_key, w_value, w_out, k_cache, v_cache, positions):
        batch, shard, kv, dim = k_cache.shape
        model = tokens.shape[1]
        groups = w_query.shape[1] // w_key.shape[1]
        heads = kv * groups
        rows = shard * kv
        flat = (batch, rows, dim)
        hspec = pl.BlockSpec(memory_space=pltpu.HBM)
        anyspec = pl.BlockSpec(memory_space=pl.ANY)
        vspec = pl.BlockSpec(memory_space=pltpu.VMEM)
        dma = pltpu.SemaphoreType.DMA
        cache = jax.ShapeDtypeStruct(flat, BF16)
        blocks = groups + 2
        proj, kb, vb = pl.pallas_call(
            functools.partial(project, groups),
            out_shape=(jax.ShapeDtypeStruct((blocks, batch, kv * dim), BF16), cache, cache),
            in_specs=[hspec] * 6,
            out_specs=(vspec,) * 3,
            scratch_shapes=[pltpu.VMEM(tokens.shape, BF16), pltpu.VMEM((4, model // 4, kv * dim), BF16), dma,
                            dma((4,)), dma((8,)), dma((8,)), dma, dma],
            compiler_params=pltpu.CompilerParams(collective_id=1, has_side_effects=True, vmem_limit_bytes=34 << 20),
            cost_estimate=pl.CostEstimate(flops=10**10, bytes_accessed=30 * 10**6, transcendentals=0),
            name='project',
        )(tokens, w_query, w_key, w_value, k_cache.reshape(flat), v_cache.reshape(flat))
        k_new, v_new, _, _, acc, stat = pl.pallas_call(
            functools.partial(attend, groups),
            out_shape=(cache, cache, cache, cache, jax.ShapeDtypeStruct((heads, batch, dim), F32),
                       jax.ShapeDtypeStruct((PAD, dim), F32)),
            in_specs=[vspec, vspec, vspec, pl.BlockSpec(memory_space=pltpu.SMEM)],
            out_specs=(hspec, hspec, vspec, vspec, vspec, vspec),
            input_output_aliases={1: 2, 2: 3},
            scratch_shapes=[pltpu.VMEM((batch * PAD, dim), F32), pltpu.VMEM((2, batch, kv * dim), F32),
                            pltpu.VMEM((batch * PAD, dim), F32), pltpu.VMEM((2, rows, NB * PAD), F32),
                            dma((2, batch // NB))],
            compiler_params=pltpu.CompilerParams(vmem_limit_bytes=24 << 20),
            cost_estimate=pl.CostEstimate(flops=10**10, bytes_accessed=17 * 10**6, transcendentals=0),
            name='attend',
        )(proj, kb, vb, positions)

        wide = model // 8
        step = batch // 2 // NC
        ns = lax.axis_size('seq')
        y = pl.pallas_call(
            finish,
            out_shape=jax.ShapeDtypeStruct((8, 8, model), BF16),
            in_specs=[vspec, vspec, anyspec],
            out_specs=vspec,
            scratch_shapes=[
                pltpu.VMEM((2 * w_out.shape[0], model), BF16),
                pltpu.VMEM((ns, NC, 2 * heads // ns, step, dim), F32),
                pltpu.VMEM((ns, 8, dim), F32),
                pltpu.VMEM((dim, dim), F32),
                pltpu.VMEM((NC, step, 2 * w_out.shape[0]), BF16),
                pltpu.VMEM((NC, 8, step, wide), F32),
                pltpu.VMEM((NC, 8, step, wide), F32),
                pltpu.VMEM((NC, 2, 4, 8, wide // 2), F32),
                pltpu.VMEM((NC, 8, 8, wide // 2), F32),
                pltpu.VMEM((8, 2, NC, 4, 8, wide // 2), BF16),
                dma, dma, dma,
                dma((NC, 8)), dma((NC, 8)), dma((8,)), dma((8,)),
            ] + [dma((NC, 8))] * 10,
            compiler_params=pltpu.CompilerParams(collective_id=0, has_side_effects=True, vmem_limit_bytes=32 << 20),
            name='finish',
        )(acc, stat, w_out)
        return y.reshape(batch, model), k_new.reshape(k_cache.shape), v_new.reshape(v_cache.shape)

    return jax.shard_map(
        local_step,
        mesh=mesh,
        in_specs=(P('rep', None), P(), P(), P(), P(('head', 'seq'), None), cache_spec, cache_spec, P('rep')),
        out_specs=(P('rep', None), cache_spec, cache_spec),
        check_vma=False,
    )
```

time: 61.2 us -> 51.6 us (0.84)
  Pallas kernels: 58.4 us -> 48.8 us
    pallas_call x1, Pallas kernels: 39.4 us -> 31.9 us  [local_step(): pl.pallas_call(finish, out_shape=jax.ShapeDtypeStruct((8, 8, model), BF16...]
    pallas_call x1, Pallas kernels: 9.37 us -> 6.83 us  [local_step(): pl.pallas_call(functools.partial(attend, groups), out_shape=(cache, cache...]
where the time goes in v3:
time: 51.6 us; the launch traced here: 51.5 us
  Pallas kernels  48.8 us (95%)
  local copies, waits for them, and re-layouts  2.02 us (4%)
  between operations  0.69 us (1%)
    pallas_call x1, Pallas kernels, local_step(): pl.pallas_call(finish, out_shape=jax.ShapeDtypeStruct((8, 8, model), BF16...  31.9 us
    pallas_call x1, Pallas kernels, local_step(): pl.pallas_call(functools.partial(project, groups), out_shape=(jax.ShapeDt...  10.1 us
    pallas_call x1, Pallas kernels, local_step(): pl.pallas_call(functools.partial(attend, groups), out_shape=(cache, cache...  6.83 us
    unnamed x7, local copies, waits for them, and re-layouts  2.02 us

profile of v3, /device:TPU:97, one launch (start us, length us, event | category | flops | bytes accessed | tf_op | source)
XLA Modules:
  0.0 51.5 jit_solution(17061335921119336534)
XLA Ops:
  0.6 0.0 copy-start.1
  0.6 1.1 %copy-done.1 = bf16[64,6144]{1,0:T(8,128)(2,1)S(1)} copy-done((bf16[64,6144]{1,0:T(8,128)(2,1)S(1)}, bf16[64,6144]{1,0:T(8,128)(2,1)}, u32[]{:S(2)}) %copy-start.1) | copy-done | bytes 786456
  1.8 0.0 copy-start.2
  1.8 10.1 %project.1 = (bf16[8,64,256]{2,1,0:T(8,128)(2,1)S(1)}, bf16[64,512,128]{2,1,0:T(8,128)(2,1)S(1)}, bf16[64,512,128]{2,1,0:T(8,128)(2,1)S(1)}) custom-call(bf16[64,6144]{1,0:T(8,128)(2,1)S(1)} %copy-done.1, bf16[6144,6144]{1,0:T(8,128)(2,1)} %wq.1, bf16[6144,1024]{1,0:T(8,128)(2,1)} %wk.1, bf16[6144,1024]{1,0:T(8,128)(2,1)} %wv.1, ...), custom_call_target="tpu_custom_call" | custom-call | flops 10000000000 | bytes 30000000 | tf_op jit(solution)/shard_map/project/pallas_call | solution.py:346
  11.8 0.0 copy-done.2
  11.8 0.0 copy-start
  11.9 6.8 %attend.1 = (bf16[64,512,128]{2,1,0:T(8,128)(2,1)}, bf16[64,512,128]{2,1,0:T(8,128)(2,1)}, bf16[64,512,128]{2,1,0:T(8,128)(2,1)S(1)}, bf16[64,512,128]{2,1,0:T(8...) custom-call(bf16[8,64,256]{2,1,0:T(8,128)(2,1)S(1)} %get-tuple-eleme, ...), custom_call_target="tpu_custom_call", output_to_operand_aliasing={{2}: (1, {}), {3}: (2, {})} | custom-call | flops 10000000000 | bytes 17000000 | tf_op jit(solution)/shard_map/attend/pallas_call | solution.py:357
  18.7 0.0 copy-done
  18.7 31.9 %finish.1 = bf16[8,8,6144]{2,1,0:T(8,128)(2,1)S(1)} custom-call(f32[12,64,128]{2,1,0:T(8,128)S(1)} %get-tuple-element.13.acch, f32[16,128]{1,0:T(8,128)S(1)} %get-tuple-element.14.stat, bf16[192,6144]{1,0:T(8,128)(2,1)S(1)} %copy-done), custom_call_target="tpu_custom_call" | custom-call | tf_op jit(solution)/shard_map/finish/pallas_call | solution.py:375
  50.6 0.9 %copy.16 = bf16[64,6144]{1,0:T(8,128)(2,1)} copy(bf16[64,6144]{1,0:T(8,128)(2,1)S(1)} %bitcast.5) | data formatting | bytes 1572864
Async XLA Ops:
  0.6 1.1 %copy-start.1 = (bf16[64,6144]{1,0:T(8,128)(2,1)S(1)}, bf16[64,6144]{1,0:T(8,128)(2,1)}, u32[]{:S(2)}) copy-start(bf16[64,6144]{1,0:T(8,128)(2,1)} %tokens.1) | copy-start | bytes 2359300
  1.8 10.1 %copy-start.2 = (s32[64]{0:T(128)S(1)}, s32[64]{0:T(128)}, u32[]{:S(2)}) copy-start(s32[64]{0:T(128)} %pos.1) | copy-start | bytes 772
  11.8 6.9 %copy-start = (bf16[192,6144]{1,0:T(8,128)(2,1)S(1)}, bf16[192,6144]{1,0:T(8,128)(2,1)}, u32[]{:S(2)}) copy-start(bf16[192,6144]{1,0:T(8,128)(2,1)} %wo.1) | copy-start | bytes 7077892

commit v4 on v3

--- a/solution.py
+++ b/solution.py
@@ -73,9 +73,6 @@
     shard = rows // 2
     heads = 2 * groups
     steps = batch // NB
-    q2[...] = jnp.zeros_like(q2)
-    for h in range(heads):
-        q2[pl.ds(h, batch, stride=PAD), :] = pj[h // 2][:, (h % 2) * dim:(h % 2 + 1) * dim].astype(F32)
     nkv[0] = pj[groups].astype(F32)
     nkv[1] = pj[groups + 1].astype(F32)
 
@@ -114,6 +111,9 @@
         return carry
 
     lax.fori_loop(0, steps, refresh, 0)
+    q2[...] = jnp.zeros_like(q2)
+    for h in range(heads):
+        q2[pl.ds(h, batch, stride=PAD), :] = pj[h // 2][:, (h % 2) * dim:(h % 2 + 1) * dim].astype(F32)
     ql = lax.broadcasted_iota(jnp.int32, (dim, lanes), 1) // PAD
 
     def scores(c):
@@ -162,7 +162,7 @@
         out(1, c).wait()
 
 
-def finish(acch, stat, wo, out, wob, rx, srx, fs, lhs, z, r1, s1, r2, yb,
+def finish(acch, stat, wo, out, wob, rx, srx, fs, lhs, z, r1, s1, r2,
            osem, w_s, w_r, d_s, d_r, t_s, t_r, a_s, a_r, b_s, b_r, c_s, c_r, e_s, e_r, f_s, f_r):
     y = lax.axis_index('head')
     s = lax.axis_index('seq')
@@ -207,6 +207,11 @@
         cp.start()
         sends.append(cp)
         return cp
+
+    def flush(n):
+        for cp in sends[:n]:
+            cp.wait_send()
+        del sends[:n]
 
     stats, parts = [], {c: [] for c in range(nc)}
     for c in range(nc):
@@ -244,6 +249,7 @@
     def order_of(side):
         return y if side == 0 else x
 
+    early = len(sends)
     cols = [fs[pl.ds(x * per + j, 8, stride=PAD), :] for j in range(per)]
     one, two, three, four, last = {}, {}, {}, {}, {c: [] for c in range(nc)}
     for c in range(nc):
@@ -283,46 +289,52 @@
                 i = base + k
                 two[c, side, k] = go(s1.at[c, side, dest], r2.at[c, i], b_s.at[c, i], b_r.at[c, i], far(side, k))
 
+    flush(early)
+
+    def piece(c, n, r=None):
+        row = 4 * p + 2 * c
+        if r is None:
+            return out.at[pl.ds(row, 2), :, pl.ds(pl.multiple_of(n * wide, wide), wide)]
+        return out.at[row + r // 2, :, pl.ds(pl.multiple_of(n * wide + lax.rem(r, 2) * short, short), short)]
+
     for c in range(nc):
         for side in range(2):
             base = side * 4
             for k in (1, 3, 2):
                 two[c, side, k].wait_recv()
             v = s1[c, side, order_of(side)] + r2[c, base + 1] + r2[c, base + 2] + r2[c, base + 3]
-            part = yb.at[block_of(side, 0), p, c, order_of(side)]
+            part = piece(c, block_of(side, 0), order_of(side))
             part[...] = v.astype(BF16)
             for k in (2, 1, 3):
                 i = base + k
                 three[c, side, k] = go(part, part, c_s.at[c, i], c_r.at[c, i], far(side, k))
 
+    flush(6 * nc)
+
     def mirror(c, side, k):
-        part = yb.at[block_of(side, 4 - k), p, c]
+        part = piece(c, block_of(side, 4 - k))
         i = side * 4 + k
         last[c].append(go(part, part, f_s.at[c, i], f_r.at[c, i], partner))
 
     for c in range(nc):
         for side in range(2):
-            part = yb.at[block_of(side, 0), p, c]
+            part = piece(c, block_of(side, 0))
             for k in (1, 3, 2):
                 three[c, side, k].wait_recv()
             for k in (2, 1, 3):
                 i = side * 4 + k
                 four[c, side, k] = go(part, part, e_s.at[c, i], e_r.at[c, i], near(side, k))
             mirror(c, side, 0)
+    flush(6 * nc)
     for c in range(nc):
         for k in (1, 3, 2):
             for side in range(2):
                 four[c, side, k].wait_recv()
                 mirror(c, side, k)
+    flush(6 * nc)
     for c in range(nc):
         for cp in last[c]:
             cp.wait_recv()
-        for n in range(2 * nx):
-            for q in range(2):
-                for r in range(4):
-                    row = q * 4 + c * 2 + r // 2
-                    left = n * wide + (r % 2) * short
-                    out[row, :, left:left + short] = yb[n, q, c, r]
     for cp in sends:
         cp.wait_send()
 
@@ -350,10 +362,11 @@
             out_specs=(vspec,) * 3,
             scratch_shapes=[pltpu.VMEM(tokens.shape, BF16), pltpu.VMEM((4, model // 4, kv * dim), BF16), dma,
                             dma((4,)), dma((8,)), dma((8,)), dma, dma],
-            compiler_params=pltpu.CompilerParams(collective_id=1, has_side_effects=True, vmem_limit_bytes=34 << 20),
+            compiler_params=pltpu.CompilerParams(collective_id=1, has_side_effects=True, vmem_limit_bytes=16 << 20),
             cost_estimate=pl.CostEstimate(flops=10**10, bytes_accessed=30 * 10**6, transcendentals=0),
             name='project',
-        )(tokens, w_query, w_key, w_value, k_cache.reshape(flat), v_cache.reshape(flat))
+        )(*[pltpu.with_memory_space_constraint(a, pltpu.HBM) for a in (
+            tokens, w_query, w_key, w_value, k_cache.reshape(flat), v_cache.reshape(flat))])
         k_new, v_new, _, _, acc, stat = pl.pallas_call(
             functools.partial(attend, groups),
             out_shape=(cache, cache, cache, cache, jax.ShapeDtypeStruct((heads, batch, dim), F32),
@@ -364,7 +377,7 @@
             scratch_shapes=[pltpu.VMEM((batch * PAD, dim), F32), pltpu.VMEM((2, batch, kv * dim), F32),
                             pltpu.VMEM((batch * PAD, dim), F32), pltpu.VMEM((2, rows, NB * PAD), F32),
                             dma((2, batch // NB))],
-            compiler_params=pltpu.CompilerParams(vmem_limit_bytes=24 << 20),
+            compiler_params=pltpu.CompilerParams(vmem_limit_bytes=12 << 20),
             cost_estimate=pl.CostEstimate(flops=10**10, bytes_accessed=17 * 10**6, transcendentals=0),
             name='attend',
         )(proj, kb, vb, positions)
@@ -387,7 +400,6 @@
                 pltpu.VMEM((NC, 8, step, wide), F32),
                 pltpu.VMEM((NC, 2, 4, 8, wide // 2), F32),
                 pltpu.VMEM((NC, 8, 8, wide // 2), F32),
-                pltpu.VMEM((8, 2, NC, 4, 8, wide // 2), BF16),
                 dma, dma, dma,
                 dma((NC, 8)), dma((NC, 8)), dma((8,)), dma((8,)),
             ] + [dma((NC, 8))] * 10,

time: 51.6 us -> 50.4 us (0.977)
  local copies, waits for them, and re-layouts: 2.02 us -> 0.89 us
    unnamed x7 -> x5, local copies, waits for them, and re-layouts: 2.02 us -> 0.89 us
    pallas_call x1, Pallas kernels: 10.1 us -> 10.8 us  [local_step(): pl.pallas_call(functools.partial(project, groups), out_shape=(jax.ShapeDt...]
    pallas_call x1, Pallas kernels: 31.9 us -> 31.3 us  [local_step(): pl.pallas_call(finish, out_shape=jax.ShapeDtypeStruct((8, 8, model), BF16...]
where the time goes in v4:
time: 50.4 us; the launch traced here: 50.3 us
  Pallas kernels  48.7 us (97%)
  local copies, waits for them, and re-layouts  0.89 us (2%)
  between operations  0.69 us (1%)
    pallas_call x1, Pallas kernels, local_step(): pl.pallas_call(finish, out_shape=jax.ShapeDtypeStruct((8, 8, model), BF16...  31.3 us
    pallas_call x1, Pallas kernels, local_step(): pl.pallas_call(functools.partial(project, groups), out_shape=(jax.ShapeDt...  10.8 us
    pallas_call x1, Pallas kernels, local_step(): pl.pallas_call(functools.partial(attend, groups), out_shape=(cache, cache...  6.62 us

profile of v4, /device:TPU:97, one launch (start us, length us, event | category | flops | bytes accessed | tf_op | source)
XLA Modules:
  0.0 50.3 jit_solution(18136725592099635187)
XLA Ops:
  0.6 0.0 copy-start.1
  0.6 10.8 %project.1 = (bf16[8,64,256]{2,1,0:T(8,128)(2,1)S(1)}, bf16[64,512,128]{2,1,0:T(8,128)(2,1)S(1)}, bf16[64,512,128]{2,1,0:T(8,128)(2,1)S(1)}) custom-call(bf16[64,6144]{1,0:T(8,128)(2,1)} %tokens.1, bf16[6144,6144]{1,0:T(8,128)(2,1)} %wq.1, bf16[6144,1024]{1,0:T(8,128)(2,1)} %wk.1, bf16[6144,1024]{1,0:T(8,128)(2,1)} %wv.1, bf16[64,512,128]{2,1,0:T(8,128)(2,1)} %bitcast.6, ...), custom_call_target="tpu_custom_call" | custom-call | flops 10000000000 | bytes 30000000 | tf_op jit(solution)/shard_map/project/pallas_call | solution.py:358
  11.5 0.0 copy-done.1
  11.5 0.0 copy-start
  11.5 6.6 %attend.1 = (bf16[64,512,128]{2,1,0:T(8,128)(2,1)}, bf16[64,512,128]{2,1,0:T(8,128)(2,1)}, bf16[64,512,128]{2,1,0:T(8,128)(2,1)S(1)}, bf16[64,512,128]{2,1,0:T(8...) custom-call(bf16[8,64,256]{2,1,0:T(8,128)(2,1)S(1)} %get-tuple-eleme, ...), custom_call_target="tpu_custom_call", output_to_operand_aliasing={{2}: (1, {}), {3}: (2, {})} | custom-call | flops 10000000000 | bytes 17000000 | tf_op jit(solution)/shard_map/attend/pallas_call | solution.py:370
  18.1 0.0 copy-done
  18.1 31.3 %finish.1 = bf16[8,8,6144]{2,1,0:T(8,128)(2,1)S(1)} custom-call(f32[12,64,128]{2,1,0:T(8,128)S(1)} %get-tuple-element.13.acch, f32[16,128]{1,0:T(8,128)S(1)} %get-tuple-element.14.stat, bf16[192,6144]{1,0:T(8,128)(2,1)S(1)} %copy-done), custom_call_target="tpu_custom_call" | custom-call | tf_op jit(solution)/shard_map/finish/pallas_call | solution.py:388
  49.4 0.9 %copy.16 = bf16[64,6144]{1,0:T(8,128)(2,1)} copy(bf16[64,6144]{1,0:T(8,128)(2,1)S(1)} %bitcast.5) | data formatting | bytes 1572864
Async XLA Ops:
  0.6 10.9 %copy-start.1 = (s32[64]{0:T(128)S(1)}, s32[64]{0:T(128)}, u32[]{:S(2)}) copy-start(s32[64]{0:T(128)} %pos.1) | copy-start | bytes 772
  11.5 6.6 %copy-start = (bf16[192,6144]{1,0:T(8,128)(2,1)S(1)}, bf16[192,6144]{1,0:T(8,128)(2,1)}, u32[]{:S(2)}) copy-start(bf16[192,6144]{1,0:T(8,128)(2,1)} %wo.1) | copy-start | bytes 7077892

commit v5 on v4

--- a/solution.py
+++ b/solution.py
@@ -12,6 +12,7 @@
 F32 = jnp.float32
 PAD = 16
 NB = 16
+NR = 8
 NC = 2
 
 
@@ -86,14 +87,14 @@
     tile = lax.broadcasted_iota(jnp.int32, (rows // 8, 8, lanes), 0) * 4
 
     def out(j, c):
-        span = pl.ds(pl.multiple_of(c * NB, NB), NB)
+        span = pl.ds(pl.multiple_of(c * NR, NR), NR)
         src, dst = ((kb, ko), (vb, vo))[j]
         return pltpu.make_async_copy(src.at[span], dst.at[span], osem.at[j, c])
 
     def refresh(c, carry):
         fresh = []
-        for i in range(NB):
-            b = c * NB + i
+        for i in range(NR):
+            b = c * NR + i
             t = pos[b] - seq * shard
             inside = (t >= 0) & (t < shard)
             tc = jnp.clip(t, 0, shard - 1)
@@ -110,7 +111,7 @@
         out(1, c).start()
         return carry
 
-    lax.fori_loop(0, steps, refresh, 0)
+    lax.fori_loop(0, batch // NR, refresh, 0)
     q2[...] = jnp.zeros_like(q2)
     for h in range(heads):
         q2[pl.ds(h, batch, stride=PAD), :] = pj[h // 2][:, (h % 2) * dim:(h % 2 + 1) * dim].astype(F32)
@@ -157,12 +158,12 @@
         mix(c)
     for h in range(heads):
         acch[h] = accs[pl.ds(h, batch, stride=PAD), :]
-    for c in range(steps):
+    for c in range(batch // NR):
         out(0, c).wait()
         out(1, c).wait()
 
 
-def finish(acch, stat, wo, out, wob, rx, srx, fs, lhs, z, r1, s1, r2,
+def finish(acch, stat, wo, out, wob, rx, srx, sx, dx, pr, fs, lhs, z, r1, s1, r2,
            osem, w_s, w_r, d_s, d_r, t_s, t_r, a_s, a_r, b_s, b_r, c_s, c_r, e_s, e_r, f_s, f_r):
     y = lax.axis_index('head')
     s = lax.axis_index('seq')
@@ -194,11 +195,11 @@
     load.start()
 
     barrier = pltpu.get_barrier_semaphore()
-    for k in range(1, ns):
-        pl.semaphore_signal(barrier, inc=1, device_id={'head': y, 'seq': lax.rem(s + k, ns)}, device_id_type=MESH)
-    for k in range(1, ny):
+    for k in (2, 1, 3):
+        pl.semaphore_signal(barrier, inc=1, device_id=on_x(k), device_id_type=MESH)
         pl.semaphore_signal(barrier, inc=1, device_id=on_y(k), device_id_type=MESH)
-    pl.semaphore_wait(barrier, ns - 1 + ny - 1)
+    pl.semaphore_signal(barrier, inc=1, device_id=partner, device_id_type=MESH)
+    pl.semaphore_wait(barrier, 7)
 
     sends = []
 
@@ -213,27 +214,46 @@
             cp.wait_send()
         del sends[:n]
 
-    stats, parts = [], {c: [] for c in range(nc)}
-    for c in range(nc):
-        for k in (4, 5, 3, 2, 6, 7, 1):
-            dest = lax.rem(s + k, ns)
-            dev = {'head': y, 'seq': dest}
-            side = lax.rem(dest, 2)
-            if c == 0:
-                rows = pl.ds(pl.multiple_of(side * 8, 8), 8)
-                stats.append(go(stat.at[rows], srx.at[k], t_s.at[k], t_r.at[k], dev))
-            rows = pl.ds(pl.multiple_of(side * half + c * step, step), step)
-            parts[c].append(go(acch.at[pl.ds((dest // 2) * per, per), rows], rx.at[k, c], d_s.at[c, k], d_r.at[c, k], dev))
+    there, here = 1 - p, p
+    scopy = go(stat.at[pl.ds(pl.multiple_of(there * 8, 8), 8)], sx, t_s.at[0], t_r.at[0], partner)
+    pairs = []
+    for c in range(nc):
+        rows = pl.ds(pl.multiple_of(there * half + c * step, step), step)
+        pairs.append(go(acch.at[:, rows], dx.at[c], d_s.at[c, 0], d_r.at[c, 0], partner))
     wcopy = go(wo, mine, w_s, w_r, partner)
-    srx[0] = stat[pl.ds(pl.multiple_of(p * 8, 8), 8)]
+    n8 = half // 8
+    fs[...] = jnp.zeros_like(fs)
+    ours = stat[pl.ds(pl.multiple_of(here * 8, 8), 8)]
+    scopy.wait_recv()
+    theirs = sx[...]
+    peak = jnp.maximum(ours[:n8], theirs[:n8])
+    base = jnp.where(peak == -jnp.inf, 0.0, peak)
+    scale = [jnp.exp(t[:n8] - base) for t in (ours, theirs)]
+    srx[0, :n8] = peak
+    srx[0, n8:] = scale[0] * ours[n8:] + scale[1] * theirs[n8:]
+    stats = [go(srx.at[0], srx.at[k], t_s.at[k], t_r.at[k], on_x(k)) for k in (2, 1, 3)]
+    fs[:n8] = scale[0]
+    fs[n8:2 * n8] = scale[1]
+    fs[...] = jnp.transpose(fs[...])
+    parts = {}
+    for c in range(nc):
+        pairs[c].wait_recv()
+        for h in range(heads):
+            col = fs[pl.ds(h, 8, stride=PAD), :]
+            for g in range(step // 8):
+                lead = c * (step // 8) + g
+                pr[c, h, 8 * g:8 * g + 8] = (col[:, lead:lead + 1] * acch[h, pl.ds(half * here + 8 * lead, 8)]
+                                             + col[:, n8 + lead:n8 + lead + 1] * dx[c, h, 8 * g:8 * g + 8])
+        parts[c] = [go(pr.at[c, pl.ds(lax.rem(x + k, nx) * per, per)], rx.at[k, c], d_s.at[c, k], d_r.at[c, k], on_x(k))
+                    for k in (2, 1, 3)]
+
     fs[...] = jnp.zeros_like(fs)
     for cp in stats:
         cp.wait_recv()
-    n8 = half // 8
-    top = functools.reduce(jnp.maximum, [srx[i, :n8] for i in range(ns)])
-    scale = [jnp.exp(srx[i, :n8] - top) for i in range(ns)]
+    top = functools.reduce(jnp.maximum, [srx[i, :n8] for i in range(nx)])
+    scale = [jnp.exp(srx[i, :n8] - top) for i in range(nx)]
     total = functools.reduce(lambda a, b: a + b, [e * srx[i, n8:] for i, e in enumerate(scale)])
-    for i in range(ns):
+    for i in range(nx):
         fs[i * n8:(i + 1) * n8, :] = scale[i] / total
     fs[...] = jnp.transpose(fs[...])
 
@@ -259,8 +279,8 @@
             rows = []
             for g in range(step // 8):
                 lead = c * (step // 8) + g
-                acc = cols[j][:, lead:lead + 1] * acch[x * per + j, pl.ds(half * p + 8 * lead, 8)]
-                for i in range(1, ns):
+                acc = cols[j][:, lead:lead + 1] * pr[c, x * per + j, 8 * g:8 * g + 8]
+                for i in range(1, nx):
                     acc = acc + cols[j][:, i * n8 + lead:i * n8 + lead + 1] * rx[i, c, j, 8 * g:8 * g + 8]
                 rows.append(acc)
             lhs[c, :, j * dim:(j + 1) * dim] = jnp.concatenate(rows, axis=0).astype(BF16)
@@ -376,7 +396,7 @@
             input_output_aliases={1: 2, 2: 3},
             scratch_shapes=[pltpu.VMEM((batch * PAD, dim), F32), pltpu.VMEM((2, batch, kv * dim), F32),
                             pltpu.VMEM((batch * PAD, dim), F32), pltpu.VMEM((2, rows, NB * PAD), F32),
-                            dma((2, batch // NB))],
+                            dma((2, batch // NR))],
             compiler_params=pltpu.CompilerParams(vmem_limit_bytes=12 << 20),
             cost_estimate=pl.CostEstimate(flops=10**10, bytes_accessed=17 * 10**6, transcendentals=0),
             name='attend',
@@ -392,8 +412,11 @@
             out_specs=vspec,
             scratch_shapes=[
                 pltpu.VMEM((2 * w_out.shape[0], model), BF16),
-                pltpu.VMEM((ns, NC, 2 * heads // ns, step, dim), F32),
-                pltpu.VMEM((ns, 8, dim), F32),
+                pltpu.VMEM((ns // 2, NC, 2 * heads // ns, step, dim), F32),
+                pltpu.VMEM((ns // 2, 8, dim), F32),
+                pltpu.VMEM((8, dim), F32),
+                pltpu.VMEM((NC, heads, step, dim), F32),
+                pltpu.VMEM((NC, heads, step, dim), F32),
                 pltpu.VMEM((dim, dim), F32),
                 pltpu.VMEM((NC, step, 2 * w_out.shape[0]), BF16),
                 pltpu.VMEM((NC, 8, step, wide), F32),

time: 50.4 us -> 50.2 us (level)
  no operation moved by 1% of the time
where the time goes in v5:
time: 50.2 us; the launch traced here: 50.1 us
  Pallas kernels  48.6 us (97%)
  local copies, waits for them, and re-layouts  0.89 us (2%)
  between operations  0.69 us (1%)
    pallas_call x1, Pallas kernels, local_step(): pl.pallas_call(finish, out_shape=jax.ShapeDtypeStruct((8, 8, model), BF16...  31.2 us
    pallas_call x1, Pallas kernels, local_step(): pl.pallas_call(functools.partial(project, groups), out_shape=(jax.ShapeDt...  10.8 us
    pallas_call x1, Pallas kernels, local_step(): pl.pallas_call(functools.partial(attend, groups), out_shape=(cache, cache...  6.58 us

profile of v5, /device:TPU:97, one launch (start us, length us, event | category | flops | bytes accessed | tf_op | source)
XLA Modules:
  0.0 50.1 jit_solution(11136417250045666885)
XLA Ops:
  0.6 0.0 copy-start.1
  0.6 10.8 %project.1 = (bf16[8,64,256]{2,1,0:T(8,128)(2,1)S(1)}, bf16[64,512,128]{2,1,0:T(8,128)(2,1)S(1)}, bf16[64,512,128]{2,1,0:T(8,128)(2,1)S(1)}) custom-call(bf16[64,6144]{1,0:T(8,128)(2,1)} %tokens.1, bf16[6144,6144]{1,0:T(8,128)(2,1)} %wq.1, bf16[6144,1024]{1,0:T(8,128)(2,1)} %wk.1, bf16[6144,1024]{1,0:T(8,128)(2,1)} %wv.1, bf16[64,512,128]{2,1,0:T(8,128)(2,1)} %bitcast.6, ...), custom_call_target="tpu_custom_call" | custom-call | flops 10000000000 | bytes 30000000 | tf_op jit(solution)/shard_map/project/pallas_call | solution.py:378
  11.5 0.0 copy-done.1
  11.5 0.0 copy-start
  11.5 6.6 %attend.1 = (bf16[64,512,128]{2,1,0:T(8,128)(2,1)}, bf16[64,512,128]{2,1,0:T(8,128)(2,1)}, bf16[64,512,128]{2,1,0:T(8,128)(2,1)S(1)}, bf16[64,512,128]{2,1,0:T(8...) custom-call(bf16[8,64,256]{2,1,0:T(8,128)(2,1)S(1)} %get-tuple-eleme, ...), custom_call_target="tpu_custom_call", output_to_operand_aliasing={{2}: (1, {}), {3}: (2, {})} | custom-call | flops 10000000000 | bytes 17000000 | tf_op jit(solution)/shard_map/attend/pallas_call | solution.py:390
  18.1 0.0 copy-done
  18.1 31.2 %finish.1 = bf16[8,8,6144]{2,1,0:T(8,128)(2,1)S(1)} custom-call(f32[12,64,128]{2,1,0:T(8,128)S(1)} %get-tuple-element.13.acch, f32[16,128]{1,0:T(8,128)S(1)} %get-tuple-element.14.stat, bf16[192,6144]{1,0:T(8,128)(2,1)S(1)} %copy-done), custom_call_target="tpu_custom_call" | custom-call | tf_op jit(solution)/shard_map/finish/pallas_call | solution.py:408
  49.3 0.9 %copy.16 = bf16[64,6144]{1,0:T(8,128)(2,1)} copy(bf16[64,6144]{1,0:T(8,128)(2,1)S(1)} %bitcast.5) | data formatting | bytes 1572864
Async XLA Ops:
  0.6 10.9 %copy-start.1 = (s32[64]{0:T(128)S(1)}, s32[64]{0:T(128)}, u32[]{:S(2)}) copy-start(s32[64]{0:T(128)} %pos.1) | copy-start | bytes 772
  11.5 6.6 %copy-start = (bf16[192,6144]{1,0:T(8,128)(2,1)S(1)}, bf16[192,6144]{1,0:T(8,128)(2,1)}, u32[]{:S(2)}) copy-start(bf16[192,6144]{1,0:T(8,128)(2,1)} %wo.1) | copy-start | bytes 7077892

commit v6 on v5

--- a/solution.py
+++ b/solution.py
@@ -16,7 +16,7 @@
 NC = 2
 
 
-def project(groups, tokens, wq, wk, wv, kc, vc, pj, kb, vb, tok, wbuf, tsem, wsem, ssem, rsem, ksem, vsem):
+def project(groups, tokens, wq, wk, wv, kc, vc, wo, pj, kb, vb, wob, tok, wbuf, tsem, wsem, ssem, rsem, ksem, vsem, osem):
     head = lax.axis_index('head')
     s = lax.axis_index('seq')
     ns = lax.axis_size('seq')
@@ -41,7 +41,10 @@
         def _():
             load(i, wv, head).start()
 
-    caches = [pltpu.make_async_copy(kc, kb, ksem), pltpu.make_async_copy(vc, vb, vsem)]
+    wrows = wo.shape[0]
+    mine = wob.at[pl.ds(pl.multiple_of(lax.rem(s, 2) * wrows, wrows), wrows), :]
+    caches = [pltpu.make_async_copy(kc, kb, ksem), pltpu.make_async_copy(vc, vb, vsem),
+              pltpu.make_async_copy(wo, mine, osem)]
     for cp in caches:
         cp.start()
     barrier = pltpu.get_barrier_semaphore()
@@ -60,6 +63,10 @@
                                           device_id={'head': head, 'seq': lax.rem(s + k, ns)}, device_id_type=MESH)
         cp.start()
         sends.append(cp)
+    cp = pltpu.make_async_remote_copy(src_ref=wo, dst_ref=mine, send_sem=ssem.at[0], recv_sem=rsem.at[0],
+                                      device_id={'head': head, 'seq': s + 1 - 2 * lax.rem(s, 2)}, device_id_type=MESH)
+    cp.start()
+    sends.append(cp)
     for cp in sends:
         cp.wait_recv()
     for cp in sends:
@@ -163,8 +170,8 @@
         out(1, c).wait()
 
 
-def finish(acch, stat, wo, out, wob, rx, srx, sx, dx, pr, fs, lhs, z, r1, s1, r2,
-           osem, w_s, w_r, d_s, d_r, t_s, t_r, a_s, a_r, b_s, b_r, c_s, c_r, e_s, e_r, f_s, f_r):
+def finish(acch, stat, wob, out, rx, srx, sx, dx, pr, fs, lhs, z, r1, s1, r2,
+           d_s, d_r, t_s, t_r, a_s, a_r, b_s, b_r, c_s, c_r, e_s, e_r, f_s, f_r):
     y = lax.axis_index('head')
     s = lax.axis_index('seq')
     ny = lax.axis_size('head')
@@ -173,7 +180,6 @@
     x = s // 2
     p = lax.rem(s, 2)
     heads, batch, dim = acch.shape
-    wrows = wo.shape[0]
     nc, per, step = rx.shape[1:4]
     half = nc * step
     wide = z.shape[-1]
@@ -190,10 +196,6 @@
                                             device_id=dev, device_id_type=MESH)
 
     partner = {'head': y, 'seq': x * 2 + 1 - p}
-    mine = wob.at[pl.ds(pl.multiple_of(p * wrows, wrows), wrows), :]
-    load = pltpu.make_async_copy(wo, mine, osem)
-    load.start()
-
     barrier = pltpu.get_barrier_semaphore()
     for k in (2, 1, 3):
         pl.semaphore_signal(barrier, inc=1, device_id=on_x(k), device_id_type=MESH)
@@ -220,7 +222,6 @@
     for c in range(nc):
         rows = pl.ds(pl.multiple_of(there * half + c * step, step), step)
         pairs.append(go(acch.at[:, rows], dx.at[c], d_s.at[c, 0], d_r.at[c, 0], partner))
-    wcopy = go(wo, mine, w_s, w_r, partner)
     n8 = half // 8
     fs[...] = jnp.zeros_like(fs)
     ours = stat[pl.ds(pl.multiple_of(here * 8, 8), 8)]
@@ -284,9 +285,6 @@
                     acc = acc + cols[j][:, i * n8 + lead:i * n8 + lead + 1] * rx[i, c, j, 8 * g:8 * g + 8]
                 rows.append(acc)
             lhs[c, :, j * dim:(j + 1) * dim] = jnp.concatenate(rows, axis=0).astype(BF16)
-        if c == 0:
-            load.wait()
-            wcopy.wait_recv()
         for k in (2, 1, 3, 0):
             for side in range(2):
                 n = block_of(side, k)
@@ -375,18 +373,19 @@
         dma = pltpu.SemaphoreType.DMA
         cache = jax.ShapeDtypeStruct(flat, BF16)
         blocks = groups + 2
-        proj, kb, vb = pl.pallas_call(
+        proj, kb, vb, wob = pl.pallas_call(
             functools.partial(project, groups),
-            out_shape=(jax.ShapeDtypeStruct((blocks, batch, kv * dim), BF16), cache, cache),
-            in_specs=[hspec] * 6,
-            out_specs=(vspec,) * 3,
+            out_shape=(jax.ShapeDtypeStruct((blocks, batch, kv * dim), BF16), cache, cache,
+                       jax.ShapeDtypeStruct((2 * w_out.shape[0], model), BF16)),
+            in_specs=[hspec] * 7,
+            out_specs=(vspec,) * 4,
             scratch_shapes=[pltpu.VMEM(tokens.shape, BF16), pltpu.VMEM((4, model // 4, kv * dim), BF16), dma,
-                            dma((4,)), dma((8,)), dma((8,)), dma, dma],
+                            dma((4,)), dma((8,)), dma((8,)), dma, dma, dma],
             compiler_params=pltpu.CompilerParams(collective_id=1, has_side_effects=True, vmem_limit_bytes=16 << 20),
             cost_estimate=pl.CostEstimate(flops=10**10, bytes_accessed=30 * 10**6, transcendentals=0),
             name='project',
         )(*[pltpu.with_memory_space_constraint(a, pltpu.HBM) for a in (
-            tokens, w_query, w_key, w_value, k_cache.reshape(flat), v_cache.reshape(flat))])
+            tokens, w_query, w_key, w_value, k_cache.reshape(flat), v_cache.reshape(flat), w_out)])
         k_new, v_new, _, _, acc, stat = pl.pallas_call(
             functools.partial(attend, groups),
             out_shape=(cache, cache, cache, cache, jax.ShapeDtypeStruct((heads, batch, dim), F32),
@@ -408,10 +407,9 @@
         y = pl.pallas_call(
             finish,
             out_shape=jax.ShapeDtypeStruct((8, 8, model), BF16),
-            in_specs=[vspec, vspec, anyspec],
+            in_specs=[vspec, vspec, vspec],
             out_specs=vspec,
             scratch_shapes=[
-                pltpu.VMEM((2 * w_out.shape[0], model), BF16),
                 pltpu.VMEM((ns // 2, NC, 2 * heads // ns, step, dim), F32),
                 pltpu.VMEM((ns // 2, 8, dim), F32),
                 pltpu.VMEM((8, dim), F32),
@@ -423,12 +421,11 @@
                 pltpu.VMEM((NC, 8, step, wide), F32),
                 pltpu.VMEM((NC, 2, 4, 8, wide // 2), F32),
                 pltpu.VMEM((NC, 8, 8, wide // 2), F32),
-                dma, dma, dma,
                 dma((NC, 8)), dma((NC, 8)), dma((8,)), dma((8,)),
             ] + [dma((NC, 8))] * 10,
             compiler_params=pltpu.CompilerParams(collective_id=0, has_side_effects=True, vmem_limit_bytes=32 << 20),
             name='finish',
-        )(acc, stat, w_out)
+        )(acc, stat, wob)
         return y.reshape(batch, model), k_new.reshape(k_cache.shape), v_new.reshape(v_cache.shape)
 
     return jax.shard_map(

time: 50.2 us -> 50.2 us (level)
  no operation moved by 1% of the time
where the time goes in v6:
time: 50.2 us; the launch traced here: 50.1 us
  Pallas kernels  48.6 us (97%)
  local copies, waits for them, and re-layouts  0.89 us (2%)
  between operations  0.67 us (1%)
    pallas_call x1, Pallas kernels, local_step(): pl.pallas_call(finish, out_shape=jax.ShapeDtypeStruct((8, 8, model), BF16...  31.1 us
    pallas_call x1, Pallas kernels, local_step(): pl.pallas_call(functools.partial(project, groups), out_shape=(jax.ShapeDt...  10.8 us
    pallas_call x1, Pallas kernels, local_step(): pl.pallas_call(functools.partial(attend, groups), out_shape=(cache, cache...  6.58 us

profile of v6, /device:TPU:97, one launch (start us, length us, event | category | flops | bytes accessed | tf_op | source)
XLA Modules:
  0.0 50.1 jit_solution(14423083866865176991)
XLA Ops:
  0.6 0.0 copy-start
  0.6 10.8 %project.1 = (bf16[8,64,256]{2,1,0:T(8,128)(2,1)S(1)}, bf16[64,512,128]{2,1,0:T(8,128)(2,1)S(1)}, bf16[64,512,128]{2,1,0:T(8,128)(2,1)S(1)}, bf16[384,6144]{1,0:T(8,128)(2,1)S(1)}) custom-call(bf16[64,6144]{1,0:T(8,128)(2,1)} %tokens.1, bf16[6144,6144]{1,0:T(8,128)(2,1)} %wq.1, bf16[6144,1024]{1,0:T(8,128)(2,1)} %wk.1, bf16[6144,1024]{1,0:T(8,128)(2,1)} %wv.1, ...), custom_call_target="tpu_custom_call" | custom-call | flops 10000000000 | bytes 30000000 | tf_op jit(solution)/shard_map/project/pallas_call | solution.py:376
  11.5 0.0 copy-done
  11.5 6.6 %attend.1 = (bf16[64,512,128]{2,1,0:T(8,128)(2,1)}, bf16[64,512,128]{2,1,0:T(8,128)(2,1)}, bf16[64,512,128]{2,1,0:T(8,128)(2,1)S(1)}, bf16[64,512,128]{2,1,0:T(8...) custom-call(bf16[8,64,256]{2,1,0:T(8,128)(2,1)S(1)} %get-tuple-eleme, ...), custom_call_target="tpu_custom_call", output_to_operand_aliasing={{2}: (1, {}), {3}: (2, {})} | custom-call | flops 10000000000 | bytes 17000000 | tf_op jit(solution)/shard_map/attend/pallas_call | solution.py:389
  18.1 31.1 %finish.1 = bf16[8,8,6144]{2,1,0:T(8,128)(2,1)S(1)} custom-call(f32[12,64,128]{2,1,0:T(8,128)S(1)} %get-tuple-element.14.acch, f32[16,128]{1,0:T(8,128)S(1)} %get-tuple-element.15.stat, bf16[384,6144]{1,0:T(8,128)(2,1)S(1)} %get-tuple-element.16.wob), custom_call_target="tpu_custom_call" | custom-call | tf_op jit(solution)/shard_map/finish/pallas_call | solution.py:407
  49.2 0.9 %copy.16 = bf16[64,6144]{1,0:T(8,128)(2,1)} copy(bf16[64,6144]{1,0:T(8,128)(2,1)S(1)} %bitcast.5) | data formatting | bytes 1572864
Async XLA Ops:
  0.6 10.9 %copy-start = (s32[64]{0:T(128)S(1)}, s32[64]{0:T(128)}, u32[]{:S(2)}) copy-start(s32[64]{0:T(128)} %pos.1) | copy-start | bytes 772
